TPU v7x, 128 devices: a whole 4x4x4 slice. The times are simulated.
128 devices in a mesh: col: 2 (over core), row: 64 (over z, y, x).
Axes of the slice: x: 4, y: 4, z: 4, core: 2. Of those that a mesh axis runs over, the one named last changes fastest.
Arguments:
- f_rhs: float32 [1536, 48, 512], P('row', 'col')
- u_init: float32 [1536, 48, 512], P('row', 'col')
- kappa_cell: float32 [1536, 48], P('row', 'col')
- solve_mats: bfloat16 [64, 2, 576, 900], P('row', 'col')
- omega_relax: float32 [], replicated
Outputs:
- output: float32 [1536, 48, 512], P('row', 'col')
All inputs are finite; a program needn't handle non-finite values.
Results may differ from a plain program's by a relative error of at most 0.00135554.
Values are sent between devices in bfloat16 or wider.
A program may use at most 1 GiB of HBM per device.

v0:
```python
import math
import jax
import jax.numpy as jnp
from jax import lax
from jax.sharding import PartitionSpec as P

SWEEPS = 6


def shift_from(values, axis_name, axis_size, from_prev):
    if from_prev:
        pair_list = [(i, i + 1) for i in range(axis_size - 1)]
    else:
        pair_list = [(i + 1, i) for i in range(axis_size - 1)]
    return lax.ppermute(values, axis_name, pair_list)


def local_faces(kappa_blk, row_count, col_count):
    from_above = shift_from(kappa_blk[-1:, :], 'row', row_count, True)
    from_below = shift_from(kappa_blk[:1, :], 'row', row_count, False)
    from_left = shift_from(kappa_blk[:, -1:], 'col', col_count, True)
    from_right = shift_from(kappa_blk[:, :1], 'col', col_count, False)
    row_pos = lax.axis_index('row')
    col_pos = lax.axis_index('col')
    inner_v = 0.5 * (kappa_blk[1:, :] + kappa_blk[:-1, :])
    inner_h = 0.5 * (kappa_blk[:, 1:] + kappa_blk[:, :-1])
    edge_n = jnp.where(row_pos == 0, kappa_blk[:1, :], 0.5 * (kappa_blk[:1, :] + from_above))
    edge_s = jnp.where(row_pos == row_count - 1, kappa_blk[-1:, :], 0.5 * (from_below + kappa_blk[-1:, :]))
    edge_w = jnp.where(col_pos == 0, kappa_blk[:, :1], 0.5 * (kappa_blk[:, :1] + from_left))
    edge_e = jnp.where(col_pos == col_count - 1, kappa_blk[:, -1:], 0.5 * (from_right + kappa_blk[:, -1:]))
    face_n = jnp.concatenate([edge_n, inner_v], axis=0)
    face_s = jnp.concatenate([inner_v, edge_s], axis=0)
    face_w = jnp.concatenate([edge_w, inner_h], axis=1)
    face_e = jnp.concatenate([inner_h, edge_e], axis=1)
    return face_n, face_s, face_w, face_e


def apply_local(values, face_set, row_count, col_count):
    face_n, face_s, face_w, face_e = face_set
    from_above = shift_from(values[-1:], 'row', row_count, True).astype(jnp.float32)
    from_below = shift_from(values[:1], 'row', row_count, False).astype(jnp.float32)
    from_left = shift_from(values[:, -1:], 'col', col_count, True).astype(jnp.float32)
    from_right = shift_from(values[:, :1], 'col', col_count, False).astype(jnp.float32)
    center = values.astype(jnp.float32)
    up_nb = jnp.concatenate([from_above, center[:-1]], axis=0)
    down_nb = jnp.concatenate([center[1:], from_below], axis=0)
    left_nb = jnp.concatenate([from_left, center[:, :-1]], axis=1)
    right_nb = jnp.concatenate([center[:, 1:], from_right], axis=1)
    diag_sum = (face_n + face_s + face_w + face_e)[:, :, None]
    return (diag_sum * center
            - face_n[:, :, None] * up_nb
            - face_s[:, :, None] * down_nb
            - face_w[:, :, None] * left_nb
            - face_e[:, :, None] * right_nb)


def extend_block(res_bf, halo_depth, row_count, col_count):
    top_strip = shift_from(res_bf[-halo_depth:], 'row', row_count, True)
    bottom_strip = shift_from(res_bf[:halo_depth], 'row', row_count, False)
    tall_ext = jnp.concatenate([top_strip, res_bf, bottom_strip], axis=0)
    left_strip = shift_from(tall_ext[:, -halo_depth:], 'col', col_count, True)
    right_strip = shift_from(tall_ext[:, :halo_depth], 'col', col_count, False)
    return jnp.concatenate([left_strip, tall_ext, right_strip], axis=1)


def solution(mesh):
    row_count = mesh.shape['row']
    col_count = mesh.shape['col']
    grid_spec = P('row', 'col', None)

    def device_fn(f_blk, u_blk, kappa_blk, mat_blk, omega_relax):
        sub_size = u_blk.shape[0]
        rhs_count = u_blk.shape[2]
        ext_cells = mat_blk.shape[3]
        ext_size = math.isqrt(ext_cells)
        halo_depth = (ext_size - sub_size) // 2
        solve_mat = mat_blk[0, 0]
        face_set = local_faces(kappa_blk, row_count, col_count)
        residual = f_blk - apply_local(u_blk, face_set, row_count, col_count)
        u_cur = u_blk
        for sweep_idx in range(SWEEPS):
            ext_block = extend_block(residual.astype(jnp.bfloat16), halo_depth, row_count, col_count)
            local_z = jnp.dot(solve_mat, ext_block.reshape(ext_cells, rhs_count), preferred_element_type=jnp.float32)
            corr_bf = local_z.astype(jnp.bfloat16).reshape(sub_size, sub_size, rhs_count)
            u_cur = u_cur + omega_relax * corr_bf.astype(jnp.float32)
            if sweep_idx < SWEEPS - 1:
                residual = residual - omega_relax * apply_local(corr_bf, face_set, row_count, col_count)
        return u_cur

    return jax.shard_map(device_fn, mesh=mesh,
                         in_specs=(grid_spec, grid_spec, P('row', 'col'), P('row', 'col', None, None), P()),
                         out_specs=grid_spec, check_vma=False)
```

profile of v0, /device:TPU:97, one launch (start us, length us, event | category | flops | bytes accessed | tf_op | source)
XLA Modules:
  0.0 264.7 jit_solution(15304193642070836856)
XLA Ops:
  0.8 6.7 %collective-permute-start.1 = (f32[1,24]{1,0:T(1,128)S(1)}, f32[1,24]{1,0:T(1,128)S(1)}, u32[]{:S(2)}, u32[]{:S(2)}) collective-permute-start(f32[1,24]{1,0:T(1,128)S(1)} %get-tuple-element.98), channel_id=1, source_target_pairs={{1,0},{2,1},{3,2},{4,3},{5,4},{6,5},{7,6},{8,7},{9,8},{10,9},{11,1... | collective-permute-start | bytes 296 | tf_op jit(solution)/shard_map/ppermute | solution.py:15
  10.3 2.8 %collective-permute-start.3 = (f32[24,1]{1,0:T(8,128)S(1)}, f32[24,1]{1,0:T(8,128)S(1)}, u32[]{:S(2)}, u32[]{:S(2)}) collective-permute-start(f32[24,1]{1,0:T(8,128)S(1)} %get-tuple-element.94), channel_id=1, source_target_pairs={{64,0},{65,1},{66,2},{67,3},{68,4},{69,5},{70,6},{71,7},{72,8},{73... | collective-permute-start | bytes 296 | tf_op jit(solution)/shard_map/ppermute | solution.py:15
  19.4 3.3 %fusion.55 = (f32[23,24,512]{2,1,0:T(8,128)}, f32[23,24,512]{2,1,0:T(8,128)}) fusion(f32[24,24,512]{2,1,0:T(8,128)} %param.6), kind=kLoop, calls=%fused_computation.126 | loop fusion | bytes 4521984 | tf_op jit(solution)/shard_map/slice | solution.py:45
  24.4 3.0 %collective-permute-start.7 = (f32[24,1,512]{2,1,0:T(1,128)S(1)}, f32[24,1,512]{2,1,0:T(1,128)S(1)}, u32[]{:S(2)}, u32[]{:S(2)}) collective-permute-start(f32[24,1,512]{2,1,0:T(1,128)S(1)} %get-tuple-element.25), channel_id=1, source_target_pairs={{64,0},{65,1},{66,2},{67,3},{68,4},{69,5},{70,6},{71,7},{72,8},{73... | collective-permute-start | bytes 147464 | tf_op jit(solution)/shard_map/ppermute | solution.py:15
  29.4 7.9 %collective-permute-start.5 = (f32[1,24,512]{2,1,0:T(8,128)S(1)}, f32[1,24,512]{2,1,0:T(8,128)S(1)}, u32[]{:S(2)}, u32[]{:S(2)}) collective-permute-start(f32[1,24,512]{2,1,0:T(8,128)S(1)} %get-tuple-element.21), channel_id=1, source_target_pairs={{1,0},{2,1},{3,2},{4,3},{5,4},{6,5},{7,6},{8,7},{9,8},{10,9},{11,1... | collective-permute-start | bytes 147464 | tf_op jit(solution)/shard_map/ppermute | solution.py:15
  38.8 3.9 %fusion.52 = (bf16[24,24,512]{2,1,0:T(8,128)(2,1)S(1)}, f32[24,24,512]{2,1,0:T(8,128)}) fusion(f32[24,24,512]{2,1,0:T(8,128)} %param.5, f32[24,1,512]{2,1,0:T(1,128)S(1)} %collective-permute-done.7, f32[24,23,512]{2,1,0:T(8,128)} %get-tuple-element.27, f32[24,24]{1,0:T(8,128)S(1)} %get-tuple-element.19, f32[24,23,512]{2,1,0:T(8,128)} %get-tuple-element.26, ...), kind=kLoop, calls=%fused_computation.124 | loop fusion | flops 4423680 | bytes 8858880 | tf_op jit(solution)/shard_map/convert_element_type | solution.py:82
  44.7 8.1 %collective-permute-start.9 = (bf16[3,24,512]{2,1,0:T(8,128)(2,1)S(1)}, bf16[3,24,512]{2,1,0:T(8,128)(2,1)S(1)}, u32[]{:S(2)}, u32[]{:S(2)}) collective-permute-start(bf16[3,24,512]{2,1,0:T(8,128)(2,1)S(1)} %get-tuple-element.91), channel_id=1, source_target_pairs={{1,0},{2,1},{3,2},{4,3},{5,4},{6,5},{7,6},{8,7},{9,8},{10,9},{11,1... | collective-permute-start | bytes 221192 | tf_op jit(solution)/shard_map/ppermute | solution.py:15
  55.6 3.1 %collective-permute-start.11 = (bf16[30,3,512]{2,1,0:T(4,128)(2,1)S(1)}, bf16[30,3,512]{2,1,0:T(4,128)(2,1)S(1)}, u32[]{:S(2)}, u32[]{:S(2)}) collective-permute-start(bf16[30,3,512]{2,1,0:T(4,128)(2,1)S(1)} %get-tuple-element.39), channel_id=1, source_target_pairs={{64,0},{65,1},{66,2},{67,3},{68,4},{69,5},{70,6},{71,7},{72,8},{73... | collective-permute-start | bytes 276488 | tf_op jit(solution)/shard_map/ppermute | solution.py:15
  63.7 8.3 %collective-permute-start.13 = (bf16[1,24,512]{2,1,0:T(8,128)(2,1)S(1)}, bf16[1,24,512]{2,1,0:T(8,128)(2,1)S(1)}, u32[]{:S(2)}, u32[]{:S(2)}) collective-permute-start(bf16[1,24,512]{2,1,0:T(8,128)(2,1)S(1)} %get-tuple-element.83), channel_id=1, source_target_pairs={{1,0},{2,1},{3,2},{4,3},{5,4},{6,5},{7,6},{8,7},{9,8},{10,9},{11,1... | collective-permute-start | bytes 73736 | tf_op jit(solution)/shard_map/ppermute | solution.py:15
  73.3 3.2 %collective-permute-start.15 = (bf16[24,1,512]{2,1,0:T(2,128)(2,1)S(1)}, bf16[24,1,512]{2,1,0:T(2,128)(2,1)S(1)}, u32[]{:S(2)}, u32[]{:S(2)}) collective-permute-start(bf16[24,1,512]{2,1,0:T(2,128)(2,1)S(1)} %get-tuple-element.87), channel_id=1, source_target_pairs={{64,0},{65,1},{66,2},{67,3},{68,4},{69,5},{70,6},{71,7},{72,8},{73... | collective-permute-start | bytes 73736 | tf_op jit(solution)/shard_map/ppermute | solution.py:15
  80.5 7.6 %collective-permute-start.17 = (bf16[3,24,512]{2,1,0:T(8,128)(2,1)S(1)}, bf16[3,24,512]{2,1,0:T(8,128)(2,1)S(1)}, u32[]{:S(2)}, u32[]{:S(2)}) collective-permute-start(bf16[3,24,512]{2,1,0:T(8,128)(2,1)S(1)} %get-tuple-element.81), channel_id=1, source_target_pairs={{1,0},{2,1},{3,2},{4,3},{5,4},{6,5},{7,6},{8,7},{9,8},{10,9},{11,1... | collective-permute-start | bytes 221192 | tf_op jit(solution)/shard_map/ppermute | solution.py:15
  90.8 3.4 %collective-permute-start.19 = (bf16[30,3,512]{2,1,0:T(4,128)(2,1)S(1)}, bf16[30,3,512]{2,1,0:T(4,128)(2,1)S(1)}, u32[]{:S(2)}, u32[]{:S(2)}) collective-permute-start(bf16[30,3,512]{2,1,0:T(4,128)(2,1)S(1)} %get-tuple-element.37), channel_id=1, source_target_pairs={{64,0},{65,1},{66,2},{67,3},{68,4},{69,5},{70,6},{71,7},{72,8},{73... | collective-permute-start | bytes 276488 | tf_op jit(solution)/shard_map/ppermute | solution.py:15
  96.7 2.2 reshape.112
  103.3 8.2 %collective-permute-start.21 = (bf16[1,24,512]{2,1,0:T(8,128)(2,1)S(1)}, bf16[1,24,512]{2,1,0:T(8,128)(2,1)S(1)}, u32[]{:S(2)}, u32[]{:S(2)}) collective-permute-start(bf16[1,24,512]{2,1,0:T(8,128)(2,1)S(1)} %get-tuple-element.73), channel_id=1, source_target_pairs={{1,0},{2,1},{3,2},{4,3},{5,4},{6,5},{7,6},{8,7},{9,8},{10,9},{11,1... | collective-permute-start | bytes 73736 | tf_op jit(solution)/shard_map/ppermute | solution.py:15
  112.8 3.2 %collective-permute-start.23 = (bf16[24,1,512]{2,1,0:T(2,128)(2,1)S(1)}, bf16[24,1,512]{2,1,0:T(2,128)(2,1)S(1)}, u32[]{:S(2)}, u32[]{:S(2)}) collective-permute-start(bf16[24,1,512]{2,1,0:T(2,128)(2,1)S(1)} %get-tuple-element.77), channel_id=1, source_target_pairs={{64,0},{65,1},{66,2},{67,3},{68,4},{69,5},{70,6},{71,7},{72,8},{73... | collective-permute-start | bytes 73736 | tf_op jit(solution)/shard_map/ppermute | solution.py:15
  120.8 7.6 %collective-permute-start.25 = (bf16[3,24,512]{2,1,0:T(8,128)(2,1)S(1)}, bf16[3,24,512]{2,1,0:T(8,128)(2,1)S(1)}, u32[]{:S(2)}, u32[]{:S(2)}) collective-permute-start(bf16[3,24,512]{2,1,0:T(8,128)(2,1)S(1)} %get-tuple-element.71), channel_id=1, source_target_pairs={{1,0},{2,1},{3,2},{4,3},{5,4},{6,5},{7,6},{8,7},{9,8},{10,9},{11,1... | collective-permute-start | bytes 221192 | tf_op jit(solution)/shard_map/ppermute | solution.py:15
  131.2 3.4 %collective-permute-start.27 = (bf16[30,3,512]{2,1,0:T(4,128)(2,1)S(1)}, bf16[30,3,512]{2,1,0:T(4,128)(2,1)S(1)}, u32[]{:S(2)}, u32[]{:S(2)}) collective-permute-start(bf16[30,3,512]{2,1,0:T(4,128)(2,1)S(1)} %get-tuple-element.35), channel_id=1, source_target_pairs={{64,0},{65,1},{66,2},{67,3},{68,4},{69,5},{70,6},{71,7},{72,8},{73... | collective-permute-start | bytes 276488 | tf_op jit(solution)/shard_map/ppermute | solution.py:15
  141.7 8.2 %collective-permute-start.29 = (bf16[1,24,512]{2,1,0:T(8,128)(2,1)S(1)}, bf16[1,24,512]{2,1,0:T(8,128)(2,1)S(1)}, u32[]{:S(2)}, u32[]{:S(2)}) collective-permute-start(bf16[1,24,512]{2,1,0:T(8,128)(2,1)S(1)} %get-tuple-element.63), channel_id=1, source_target_pairs={{1,0},{2,1},{3,2},{4,3},{5,4},{6,5},{7,6},{8,7},{9,8},{10,9},{11,1... | collective-permute-start | bytes 73736 | tf_op jit(solution)/shard_map/ppermute | solution.py:15
  151.3 3.2 %collective-permute-start.31 = (bf16[24,1,512]{2,1,0:T(2,128)(2,1)S(1)}, bf16[24,1,512]{2,1,0:T(2,128)(2,1)S(1)}, u32[]{:S(2)}, u32[]{:S(2)}) collective-permute-start(bf16[24,1,512]{2,1,0:T(2,128)(2,1)S(1)} %get-tuple-element.67), channel_id=1, source_target_pairs={{64,0},{65,1},{66,2},{67,3},{68,4},{69,5},{70,6},{71,7},{72,8},{73... | collective-permute-start | bytes 73736 | tf_op jit(solution)/shard_map/ppermute | solution.py:15
  159.4 7.6 %collective-permute-start.33 = (bf16[3,24,512]{2,1,0:T(8,128)(2,1)S(1)}, bf16[3,24,512]{2,1,0:T(8,128)(2,1)S(1)}, u32[]{:S(2)}, u32[]{:S(2)}) collective-permute-start(bf16[3,24,512]{2,1,0:T(8,128)(2,1)S(1)} %get-tuple-element.61), channel_id=1, source_target_pairs={{1,0},{2,1},{3,2},{4,3},{5,4},{6,5},{7,6},{8,7},{9,8},{10,9},{11,1... | collective-permute-start | bytes 221192 | tf_op jit(solution)/shard_map/ppermute | solution.py:15
  169.8 3.4 %collective-permute-start.35 = (bf16[30,3,512]{2,1,0:T(4,128)(2,1)S(1)}, bf16[30,3,512]{2,1,0:T(4,128)(2,1)S(1)}, u32[]{:S(2)}, u32[]{:S(2)}) collective-permute-start(bf16[30,3,512]{2,1,0:T(4,128)(2,1)S(1)} %get-tuple-element.33), channel_id=1, source_target_pairs={{64,0},{65,1},{66,2},{67,3},{68,4},{69,5},{70,6},{71,7},{72,8},{73... | collective-permute-start | bytes 276488 | tf_op jit(solution)/shard_map/ppermute | solution.py:15
  175.7 2.2 reshape.116
  182.2 8.2 %collective-permute-start.37 = (bf16[1,24,512]{2,1,0:T(8,128)(2,1)S(1)}, bf16[1,24,512]{2,1,0:T(8,128)(2,1)S(1)}, u32[]{:S(2)}, u32[]{:S(2)}) collective-permute-start(bf16[1,24,512]{2,1,0:T(8,128)(2,1)S(1)} %get-tuple-element.53), channel_id=1, source_target_pairs={{1,0},{2,1},{3,2},{4,3},{5,4},{6,5},{7,6},{8,7},{9,8},{10,9},{11,1... | collective-permute-start | bytes 73736 | tf_op jit(solution)/shard_map/ppermute | solution.py:15
  191.8 3.2 %collective-permute-start.39 = (bf16[24,1,512]{2,1,0:T(2,128)(2,1)S(1)}, bf16[24,1,512]{2,1,0:T(2,128)(2,1)S(1)}, u32[]{:S(2)}, u32[]{:S(2)}) collective-permute-start(bf16[24,1,512]{2,1,0:T(2,128)(2,1)S(1)} %get-tuple-element.57), channel_id=1, source_target_pairs={{64,0},{65,1},{66,2},{67,3},{68,4},{69,5},{70,6},{71,7},{72,8},{73... | collective-permute-start | bytes 73736 | tf_op jit(solution)/shard_map/ppermute | solution.py:15
  199.7 7.6 %collective-permute-start.41 = (bf16[3,24,512]{2,1,0:T(8,128)(2,1)S(1)}, bf16[3,24,512]{2,1,0:T(8,128)(2,1)S(1)}, u32[]{:S(2)}, u32[]{:S(2)}) collective-permute-start(bf16[3,24,512]{2,1,0:T(8,128)(2,1)S(1)} %get-tuple-element.51), channel_id=1, source_target_pairs={{1,0},{2,1},{3,2},{4,3},{5,4},{6,5},{7,6},{8,7},{9,8},{10,9},{11,1... | collective-permute-start | bytes 221192 | tf_op jit(solution)/shard_map/ppermute | solution.py:15
  210.1 3.4 %collective-permute-start.43 = (bf16[30,3,512]{2,1,0:T(4,128)(2,1)S(1)}, bf16[30,3,512]{2,1,0:T(4,128)(2,1)S(1)}, u32[]{:S(2)}, u32[]{:S(2)}) collective-permute-start(bf16[30,3,512]{2,1,0:T(4,128)(2,1)S(1)} %get-tuple-element.31), channel_id=1, source_target_pairs={{64,0},{65,1},{66,2},{67,3},{68,4},{69,5},{70,6},{71,7},{72,8},{73... | collective-permute-start | bytes 276488 | tf_op jit(solution)/shard_map/ppermute | solution.py:15
  220.6 8.2 %collective-permute-start.45 = (bf16[1,24,512]{2,1,0:T(8,128)(2,1)S(1)}, bf16[1,24,512]{2,1,0:T(8,128)(2,1)S(1)}, u32[]{:S(2)}, u32[]{:S(2)}) collective-permute-start(bf16[1,24,512]{2,1,0:T(8,128)(2,1)S(1)} %get-tuple-element.48), channel_id=1, source_target_pairs={{1,0},{2,1},{3,2},{4,3},{5,4},{6,5},{7,6},{8,7},{9,8},{10,9},{11,1... | collective-permute-start | bytes 73736 | tf_op jit(solution)/shard_map/ppermute | solution.py:15
  230.8 2.5 collective-permute-start.47
  235.1 2.5 collective-permute-done.44
  240.9 7.6 %collective-permute-start.49 = (bf16[3,24,512]{2,1,0:T(8,128)(2,1)S(1)}, bf16[3,24,512]{2,1,0:T(8,128)(2,1)S(1)}, u32[]{:S(2)}, u32[]{:S(2)}) collective-permute-start(bf16[3,24,512]{2,1,0:T(8,128)(2,1)S(1)} %get-tuple-element.41), channel_id=1, source_target_pairs={{1,0},{2,1},{3,2},{4,3},{5,4},{6,5},{7,6},{8,7},{9,8},{10,9},{11,1... | collective-permute-start | bytes 221192 | tf_op jit(solution)/shard_map/ppermute | solution.py:15
  251.3 4.8 %collective-permute-start.51 = (bf16[30,3,512]{2,1,0:T(4,128)(2,1)S(1)}, bf16[30,3,512]{2,1,0:T(4,128)(2,1)S(1)}, u32[]{:S(2)}, u32[]{:S(2)}) collective-permute-start(bf16[30,3,512]{2,1,0:T(4,128)(2,1)S(1)} %get-tuple-element.29), channel_id=1, source_target_pairs={{64,0},{65,1},{66,2},{67,3},{68,4},{69,5},{70,6},{71,7},{72,8},{73... | collective-permute-start | bytes 276488 | tf_op jit(solution)/shard_map/ppermute | solution.py:15
  258.5 2.2 reshape.120
  (204 shorter events, 102.0 us)
Async XLA Ops:
  0.8 23.6 %collective-permute-start.1 = (f32[1,24]{1,0:T(1,128)S(1)}, f32[1,24]{1,0:T(1,128)S(1)}, u32[]{:S(2)}, u32[]{:S(2)}) collective-permute-start(f32[1,24]{1,0:T(1,128)S(1)} %get-tuple-element.98), channel_id=1, source_target_pairs={{1,0},{2,1},{3,2},{4,3},{5,4},{6,5},{7,6},{8,7},{9,8},{10,9},{11,1... | collective-permute-start | bytes 296 | tf_op jit(solution)/shard_map/ppermute | solution.py:15
  7.5 19.9 %collective-permute-start = (f32[1,24]{1,0:T(1,128)S(1)}, f32[1,24]{1,0:T(1,128)S(1)}, u32[]{:S(2)}, u32[]{:S(2)}) collective-permute-start(f32[1,24]{1,0:T(1,128)S(1)} %get-tuple-element.99), channel_id=1, source_target_pairs={{0,1},{1,2},{2,3},{3,4},{4,5},{5,6},{6,7},{7,8},{8,9},{9,10},{10,1... | collective-permute-start | bytes 296 | tf_op jit(solution)/shard_map/ppermute | solution.py:15
  10.3 19.1 %collective-permute-start.3 = (f32[24,1]{1,0:T(8,128)S(1)}, f32[24,1]{1,0:T(8,128)S(1)}, u32[]{:S(2)}, u32[]{:S(2)}) collective-permute-start(f32[24,1]{1,0:T(8,128)S(1)} %get-tuple-element.94), channel_id=1, source_target_pairs={{64,0},{65,1},{66,2},{67,3},{68,4},{69,5},{70,6},{71,7},{72,8},{73... | collective-permute-start | bytes 296 | tf_op jit(solution)/shard_map/ppermute | solution.py:15
  13.1 24.1 %collective-permute-start.2 = (f32[24,1]{1,0:T(8,128)S(1)}, f32[24,1]{1,0:T(8,128)S(1)}, u32[]{:S(2)}, u32[]{:S(2)}) collective-permute-start(f32[24,1]{1,0:T(8,128)S(1)} %get-tuple-element.95), channel_id=1, source_target_pairs={{0,64},{1,65},{2,66},{3,67},{4,68},{5,69},{6,70},{7,71},{8,72},{9,... | collective-permute-start | bytes 296 | tf_op jit(solution)/shard_map/ppermute | solution.py:15
  15.6 21.8 %collective-permute-start.6 = (f32[24,1,512]{2,1,0:T(1,128)S(1)}, f32[24,1,512]{2,1,0:T(1,128)S(1)}, u32[]{:S(2)}, u32[]{:S(2)}) collective-permute-start(f32[24,1,512]{2,1,0:T(1,128)S(1)} %get-tuple-element.24), channel_id=1, source_target_pairs={{0,64},{1,65},{2,66},{3,67},{4,68},{5,69},{6,70},{7,71},{8,72},{9,... | collective-permute-start | bytes 147464 | tf_op jit(solution)/shard_map/ppermute | solution.py:15
  24.4 13.1 %collective-permute-start.7 = (f32[24,1,512]{2,1,0:T(1,128)S(1)}, f32[24,1,512]{2,1,0:T(1,128)S(1)}, u32[]{:S(2)}, u32[]{:S(2)}) collective-permute-start(f32[24,1,512]{2,1,0:T(1,128)S(1)} %get-tuple-element.25), channel_id=1, source_target_pairs={{64,0},{65,1},{66,2},{67,3},{68,4},{69,5},{70,6},{71,7},{72,8},{73... | collective-permute-start | bytes 147464 | tf_op jit(solution)/shard_map/ppermute | solution.py:15
  27.4 10.0 %collective-permute-start.4 = (f32[1,24,512]{2,1,0:T(8,128)S(1)}, f32[1,24,512]{2,1,0:T(8,128)S(1)}, u32[]{:S(2)}, u32[]{:S(2)}) collective-permute-start(f32[1,24,512]{2,1,0:T(8,128)S(1)} %get-tuple-element.20), channel_id=1, source_target_pairs={{0,1},{1,2},{2,3},{3,4},{4,5},{5,6},{6,7},{7,8},{8,9},{9,10},{10,1... | collective-permute-start | bytes 147464 | tf_op jit(solution)/shard_map/ppermute | solution.py:15
  29.4 9.5 %collective-permute-start.5 = (f32[1,24,512]{2,1,0:T(8,128)S(1)}, f32[1,24,512]{2,1,0:T(8,128)S(1)}, u32[]{:S(2)}, u32[]{:S(2)}) collective-permute-start(f32[1,24,512]{2,1,0:T(8,128)S(1)} %get-tuple-element.21), channel_id=1, source_target_pairs={{1,0},{2,1},{3,2},{4,3},{5,4},{6,5},{7,6},{8,7},{9,8},{10,9},{11,1... | collective-permute-start | bytes 147464 | tf_op jit(solution)/shard_map/ppermute | solution.py:15
  42.8 10.4 %collective-permute-start.8 = (bf16[3,24,512]{2,1,0:T(8,128)(2,1)S(1)}, bf16[3,24,512]{2,1,0:T(8,128)(2,1)S(1)}, u32[]{:S(2)}, u32[]{:S(2)}) collective-permute-start(bf16[3,24,512]{2,1,0:T(8,128)(2,1)S(1)} %get-tuple-element.90), channel_id=1, source_target_pairs={{0,1},{1,2},{2,3},{3,4},{4,5},{5,6},{6,7},{7,8},{8,9},{9,10},{10,1... | collective-permute-start | bytes 221192 | tf_op jit(solution)/shard_map/ppermute | solution.py:15
  44.7 9.5 %collective-permute-start.9 = (bf16[3,24,512]{2,1,0:T(8,128)(2,1)S(1)}, bf16[3,24,512]{2,1,0:T(8,128)(2,1)S(1)}, u32[]{:S(2)}, u32[]{:S(2)}) collective-permute-start(bf16[3,24,512]{2,1,0:T(8,128)(2,1)S(1)} %get-tuple-element.91), channel_id=1, source_target_pairs={{1,0},{2,1},{3,2},{4,3},{5,4},{6,5},{7,6},{8,7},{9,8},{10,9},{11,1... | collective-permute-start | bytes 221192 | tf_op jit(solution)/shard_map/ppermute | solution.py:15
  61.8 15.0 %collective-permute-start.12 = (bf16[1,24,512]{2,1,0:T(8,128)(2,1)S(1)}, bf16[1,24,512]{2,1,0:T(8,128)(2,1)S(1)}, u32[]{:S(2)}, u32[]{:S(2)}) collective-permute-start(bf16[1,24,512]{2,1,0:T(8,128)(2,1)S(1)} %get-tuple-element.82), channel_id=1, source_target_pairs={{0,1},{1,2},{2,3},{3,4},{4,5},{5,6},{6,7},{7,8},{8,9},{9,10},{10,1... | collective-permute-start | bytes 73736 | tf_op jit(solution)/shard_map/ppermute | solution.py:15
  63.7 13.1 %collective-permute-start.13 = (bf16[1,24,512]{2,1,0:T(8,128)(2,1)S(1)}, bf16[1,24,512]{2,1,0:T(8,128)(2,1)S(1)}, u32[]{:S(2)}, u32[]{:S(2)}) collective-permute-start(bf16[1,24,512]{2,1,0:T(8,128)(2,1)S(1)} %get-tuple-element.83), channel_id=1, source_target_pairs={{1,0},{2,1},{3,2},{4,3},{5,4},{6,5},{7,6},{8,7},{9,8},{10,9},{11,1... | collective-permute-start | bytes 73736 | tf_op jit(solution)/shard_map/ppermute | solution.py:15
  78.5 9.5 %collective-permute-start.16 = (bf16[3,24,512]{2,1,0:T(8,128)(2,1)S(1)}, bf16[3,24,512]{2,1,0:T(8,128)(2,1)S(1)}, u32[]{:S(2)}, u32[]{:S(2)}) collective-permute-start(bf16[3,24,512]{2,1,0:T(8,128)(2,1)S(1)} %get-tuple-element.80), channel_id=1, source_target_pairs={{0,1},{1,2},{2,3},{3,4},{4,5},{5,6},{6,7},{7,8},{8,9},{9,10},{10,1... | collective-permute-start | bytes 221192 | tf_op jit(solution)/shard_map/ppermute | solution.py:15
  80.5 9.0 %collective-permute-start.17 = (bf16[3,24,512]{2,1,0:T(8,128)(2,1)S(1)}, bf16[3,24,512]{2,1,0:T(8,128)(2,1)S(1)}, u32[]{:S(2)}, u32[]{:S(2)}) collective-permute-start(bf16[3,24,512]{2,1,0:T(8,128)(2,1)S(1)} %get-tuple-element.81), channel_id=1, source_target_pairs={{1,0},{2,1},{3,2},{4,3},{5,4},{6,5},{7,6},{8,7},{9,8},{10,9},{11,1... | collective-permute-start | bytes 221192 | tf_op jit(solution)/shard_map/ppermute | solution.py:15
  101.4 14.9 %collective-permute-start.20 = (bf16[1,24,512]{2,1,0:T(8,128)(2,1)S(1)}, bf16[1,24,512]{2,1,0:T(8,128)(2,1)S(1)}, u32[]{:S(2)}, u32[]{:S(2)}) collective-permute-start(bf16[1,24,512]{2,1,0:T(8,128)(2,1)S(1)} %get-tuple-element.72), channel_id=1, source_target_pairs={{0,1},{1,2},{2,3},{3,4},{4,5},{5,6},{6,7},{7,8},{8,9},{9,10},{10,1... | collective-permute-start | bytes 73736 | tf_op jit(solution)/shard_map/ppermute | solution.py:15
  103.3 13.0 %collective-permute-start.21 = (bf16[1,24,512]{2,1,0:T(8,128)(2,1)S(1)}, bf16[1,24,512]{2,1,0:T(8,128)(2,1)S(1)}, u32[]{:S(2)}, u32[]{:S(2)}) collective-permute-start(bf16[1,24,512]{2,1,0:T(8,128)(2,1)S(1)} %get-tuple-element.73), channel_id=1, source_target_pairs={{1,0},{2,1},{3,2},{4,3},{5,4},{6,5},{7,6},{8,7},{9,8},{10,9},{11,1... | collective-permute-start | bytes 73736 | tf_op jit(solution)/shard_map/ppermute | solution.py:15
  118.9 9.5 %collective-permute-start.24 = (bf16[3,24,512]{2,1,0:T(8,128)(2,1)S(1)}, bf16[3,24,512]{2,1,0:T(8,128)(2,1)S(1)}, u32[]{:S(2)}, u32[]{:S(2)}) collective-permute-start(bf16[3,24,512]{2,1,0:T(8,128)(2,1)S(1)} %get-tuple-element.70), channel_id=1, source_target_pairs={{0,1},{1,2},{2,3},{3,4},{4,5},{5,6},{6,7},{7,8},{8,9},{9,10},{10,1... | collective-permute-start | bytes 221192 | tf_op jit(solution)/shard_map/ppermute | solution.py:15
  120.8 9.0 %collective-permute-start.25 = (bf16[3,24,512]{2,1,0:T(8,128)(2,1)S(1)}, bf16[3,24,512]{2,1,0:T(8,128)(2,1)S(1)}, u32[]{:S(2)}, u32[]{:S(2)}) collective-permute-start(bf16[3,24,512]{2,1,0:T(8,128)(2,1)S(1)} %get-tuple-element.71), channel_id=1, source_target_pairs={{1,0},{2,1},{3,2},{4,3},{5,4},{6,5},{7,6},{8,7},{9,8},{10,9},{11,1... | collective-permute-start | bytes 221192 | tf_op jit(solution)/shard_map/ppermute | solution.py:15
  139.8 14.9 %collective-permute-start.28 = (bf16[1,24,512]{2,1,0:T(8,128)(2,1)S(1)}, bf16[1,24,512]{2,1,0:T(8,128)(2,1)S(1)}, u32[]{:S(2)}, u32[]{:S(2)}) collective-permute-start(bf16[1,24,512]{2,1,0:T(8,128)(2,1)S(1)} %get-tuple-element.62), channel_id=1, source_target_pairs={{0,1},{1,2},{2,3},{3,4},{4,5},{5,6},{6,7},{7,8},{8,9},{9,10},{10,1... | collective-permute-start | bytes 73736 | tf_op jit(solution)/shard_map/ppermute | solution.py:15
  141.7 13.0 %collective-permute-start.29 = (bf16[1,24,512]{2,1,0:T(8,128)(2,1)S(1)}, bf16[1,24,512]{2,1,0:T(8,128)(2,1)S(1)}, u32[]{:S(2)}, u32[]{:S(2)}) collective-permute-start(bf16[1,24,512]{2,1,0:T(8,128)(2,1)S(1)} %get-tuple-element.63), channel_id=1, source_target_pairs={{1,0},{2,1},{3,2},{4,3},{5,4},{6,5},{7,6},{8,7},{9,8},{10,9},{11,1... | collective-permute-start | bytes 73736 | tf_op jit(solution)/shard_map/ppermute | solution.py:15
  157.3 9.7 %collective-permute-start.32 = (bf16[3,24,512]{2,1,0:T(8,128)(2,1)S(1)}, bf16[3,24,512]{2,1,0:T(8,128)(2,1)S(1)}, u32[]{:S(2)}, u32[]{:S(2)}) collective-permute-start(bf16[3,24,512]{2,1,0:T(8,128)(2,1)S(1)} %get-tuple-element.60), channel_id=1, source_target_pairs={{0,1},{1,2},{2,3},{3,4},{4,5},{5,6},{6,7},{7,8},{8,9},{9,10},{10,1... | collective-permute-start | bytes 221192 | tf_op jit(solution)/shard_map/ppermute | solution.py:15
  159.4 9.0 %collective-permute-start.33 = (bf16[3,24,512]{2,1,0:T(8,128)(2,1)S(1)}, bf16[3,24,512]{2,1,0:T(8,128)(2,1)S(1)}, u32[]{:S(2)}, u32[]{:S(2)}) collective-permute-start(bf16[3,24,512]{2,1,0:T(8,128)(2,1)S(1)} %get-tuple-element.61), channel_id=1, source_target_pairs={{1,0},{2,1},{3,2},{4,3},{5,4},{6,5},{7,6},{8,7},{9,8},{10,9},{11,1... | collective-permute-start | bytes 221192 | tf_op jit(solution)/shard_map/ppermute | solution.py:15
  180.3 14.9 %collective-permute-start.36 = (bf16[1,24,512]{2,1,0:T(8,128)(2,1)S(1)}, bf16[1,24,512]{2,1,0:T(8,128)(2,1)S(1)}, u32[]{:S(2)}, u32[]{:S(2)}) collective-permute-start(bf16[1,24,512]{2,1,0:T(8,128)(2,1)S(1)} %get-tuple-element.52), channel_id=1, source_target_pairs={{0,1},{1,2},{2,3},{3,4},{4,5},{5,6},{6,7},{7,8},{8,9},{9,10},{10,1... | collective-permute-start | bytes 73736 | tf_op jit(solution)/shard_map/ppermute | solution.py:15
  182.2 13.0 %collective-permute-start.37 = (bf16[1,24,512]{2,1,0:T(8,128)(2,1)S(1)}, bf16[1,24,512]{2,1,0:T(8,128)(2,1)S(1)}, u32[]{:S(2)}, u32[]{:S(2)}) collective-permute-start(bf16[1,24,512]{2,1,0:T(8,128)(2,1)S(1)} %get-tuple-element.53), channel_id=1, source_target_pairs={{1,0},{2,1},{3,2},{4,3},{5,4},{6,5},{7,6},{8,7},{9,8},{10,9},{11,1... | collective-permute-start | bytes 73736 | tf_op jit(solution)/shard_map/ppermute | solution.py:15
  197.8 9.5 %collective-permute-start.40 = (bf16[3,24,512]{2,1,0:T(8,128)(2,1)S(1)}, bf16[3,24,512]{2,1,0:T(8,128)(2,1)S(1)}, u32[]{:S(2)}, u32[]{:S(2)}) collective-permute-start(bf16[3,24,512]{2,1,0:T(8,128)(2,1)S(1)} %get-tuple-element.50), channel_id=1, source_target_pairs={{0,1},{1,2},{2,3},{3,4},{4,5},{5,6},{6,7},{7,8},{8,9},{9,10},{10,1... | collective-permute-start | bytes 221192 | tf_op jit(solution)/shard_map/ppermute | solution.py:15
  199.7 9.0 %collective-permute-start.41 = (bf16[3,24,512]{2,1,0:T(8,128)(2,1)S(1)}, bf16[3,24,512]{2,1,0:T(8,128)(2,1)S(1)}, u32[]{:S(2)}, u32[]{:S(2)}) collective-permute-start(bf16[3,24,512]{2,1,0:T(8,128)(2,1)S(1)} %get-tuple-element.51), channel_id=1, source_target_pairs={{1,0},{2,1},{3,2},{4,3},{5,4},{6,5},{7,6},{8,7},{9,8},{10,9},{11,1... | collective-permute-start | bytes 221192 | tf_op jit(solution)/shard_map/ppermute | solution.py:15
  220.6 14.5 %collective-permute-start.45 = (bf16[1,24,512]{2,1,0:T(8,128)(2,1)S(1)}, bf16[1,24,512]{2,1,0:T(8,128)(2,1)S(1)}, u32[]{:S(2)}, u32[]{:S(2)}) collective-permute-start(bf16[1,24,512]{2,1,0:T(8,128)(2,1)S(1)} %get-tuple-element.48), channel_id=1, source_target_pairs={{1,0},{2,1},{3,2},{4,3},{5,4},{6,5},{7,6},{8,7},{9,8},{10,9},{11,1... | collective-permute-start | bytes 73736 | tf_op jit(solution)/shard_map/ppermute | solution.py:15
  228.9 8.8 %collective-permute-start.44 = (bf16[1,24,512]{2,1,0:T(8,128)(2,1)S(1)}, bf16[1,24,512]{2,1,0:T(8,128)(2,1)S(1)}, u32[]{:S(2)}, u32[]{:S(2)}) collective-permute-start(bf16[1,24,512]{2,1,0:T(8,128)(2,1)S(1)} %get-tuple-element.49), channel_id=1, source_target_pairs={{0,1},{1,2},{2,3},{3,4},{4,5},{5,6},{6,7},{7,8},{8,9},{9,10},{10,1... | collective-permute-start | bytes 73736 | tf_op jit(solution)/shard_map/ppermute | solution.py:15
  230.8 6.9 %collective-permute-start.47 = (bf16[24,1,512]{2,1,0:T(2,128)(2,1)S(1)}, bf16[24,1,512]{2,1,0:T(2,128)(2,1)S(1)}, u32[]{:S(2)}, u32[]{:S(2)}) collective-permute-start(bf16[24,1,512]{2,1,0:T(2,128)(2,1)S(1)} %get-tuple-element.44), channel_id=1, source_target_pairs={{64,0},{65,1},{66,2},{67,3},{68,4},{69,5},{70,6},{71,7},{72,8},{73... | collective-permute-start | bytes 73736 | tf_op jit(solution)/shard_map/ppermute | solution.py:15
  238.9 9.5 %collective-permute-start.48 = (bf16[3,24,512]{2,1,0:T(8,128)(2,1)S(1)}, bf16[3,24,512]{2,1,0:T(8,128)(2,1)S(1)}, u32[]{:S(2)}, u32[]{:S(2)}) collective-permute-start(bf16[3,24,512]{2,1,0:T(8,128)(2,1)S(1)} %get-tuple-element.40), channel_id=1, source_target_pairs={{0,1},{1,2},{2,3},{3,4},{4,5},{5,6},{6,7},{7,8},{8,9},{9,10},{10,1... | collective-permute-start | bytes 221192 | tf_op jit(solution)/shard_map/ppermute | solution.py:15
  240.9 9.0 %collective-permute-start.49 = (bf16[3,24,512]{2,1,0:T(8,128)(2,1)S(1)}, bf16[3,24,512]{2,1,0:T(8,128)(2,1)S(1)}, u32[]{:S(2)}, u32[]{:S(2)}) collective-permute-start(bf16[3,24,512]{2,1,0:T(8,128)(2,1)S(1)} %get-tuple-element.41), channel_id=1, source_target_pairs={{1,0},{2,1},{3,2},{4,3},{5,4},{6,5},{7,6},{8,7},{9,8},{10,9},{11,1... | collective-permute-start | bytes 221192 | tf_op jit(solution)/shard_map/ppermute | solution.py:15
  250.0 6.1 %collective-permute-start.50 = (bf16[30,3,512]{2,1,0:T(4,128)(2,1)S(1)}, bf16[30,3,512]{2,1,0:T(4,128)(2,1)S(1)}, u32[]{:S(2)}, u32[]{:S(2)}) collective-permute-start(bf16[30,3,512]{2,1,0:T(4,128)(2,1)S(1)} %get-tuple-element.28), channel_id=1, source_target_pairs={{0,64},{1,65},{2,66},{3,67},{4,68},{5,69},{6,70},{7,71},{8,72},{9,... | collective-permute-start | bytes 276488 | tf_op jit(solution)/shard_map/ppermute | solution.py:15
  (42 other events, 252.7 us)
where the time goes:
time: 268 us; the launch traced here: 265 us
  starting transfers between devices  186 us (69%)
  other arithmetic  23.9 us (9%)
  local copies, waits for them, and re-layouts  22.5 us (8%)
  waiting for transfers between devices  19.1 us (7%)
  matrix products  11 us (4%)
    ppermute x52, starting transfers between devices, shift_from(): return lax.ppermute(values, axis_name, pair_list)  186 us
    ppermute x52, waiting for transfers between devices, shift_from(): return lax.ppermute(values, axis_name, pair_list)  19.1 us
    convert_element_type x6, other arithmetic, device_fn(): residual.astype(jnp.bfloat16)  11.9 us
    dot_general x6, matrix products, device_fn(): jnp.dot(solve_mat, ext_block.reshape(ext_cells, rhs_count), preferred_ele...  11 us
    reshape x6, local copies, waits for them, and re-layouts, device_fn(): ext_block.reshape(ext_cells, rhs_count)  10.3 us
    concatenate x6, other arithmetic, extend_block(): return jnp.concatenate([left_strip, tall_ext, right_strip], axis=1)  7.23 us
  transfers between devices with their start and end apart: 52, of which 19 were waited for; matrix products, arithmetic and copies ran while one was open for 4% of the time, Pallas kernels for 0%

commit v1 on v0

v1 whole, which is shorter than its diff:
```python
import functools
import math

import jax
import jax.numpy as jnp
from jax import lax
from jax.experimental import pallas as pl
from jax.experimental.pallas import tpu as pltpu
from jax.sharding import PartitionSpec as P

SWEEPS = 6
LANES = 128
MESH = pl.DeviceIdType.MESH
F32 = jnp.float32
BF16 = jnp.bfloat16


def kernel(row_count, sub, halo, chunks,
           om_ref, f_hbm, u_hbm, kap_hbm, mat_hbm, out_hbm,
           u_sc, r_sc, v_sc, e_late, e_early, acc, m_raw, m_perm,
           k_raw, kb, fv, fw, fe, dg, i_send, i_recv, z_send, z_recv,
           load_sem, pair_send, pair_recv, mat_sem, kap_loc, kap_send, kap_recv,
           is_sem, ir_sem, zs_sem, zr_sem, out_loc, out_send, out_recv):
    wide = 2 * sub
    ext = sub + 2 * halo
    band = halo + 1
    late_k = 2 * band * 32
    early_rows = e_early.shape[1]
    half = chunks * LANES
    left = 8

    row = lax.axis_index('row')
    col = lax.axis_index('col')
    other = 1 - col
    has_up = row > 0
    has_dn = row < row_count - 1
    up_row = jnp.maximum(row - 1, 0)
    dn_row = jnp.minimum(row + 1, row_count - 1)
    my_cols = pl.ds(pl.multiple_of(col * sub, 8), sub)
    other_cols = pl.ds(pl.multiple_of(other * sub, 8), sub)

    def lanes_of(which, ch):
        return pl.ds(pl.multiple_of(which * half + ch * LANES, LANES), LANES)

    barrier = pltpu.get_barrier_semaphore()

    def greet(r_to, c_to):
        pl.semaphore_signal(barrier, inc=1, device_id=(c_to, r_to), device_id_type=MESH)

    greet(row, other)

    @pl.when(has_up)
    def _():
        greet(up_row, col)
        greet(up_row, other)

    @pl.when(has_dn)
    def _():
        greet(dn_row, col)
        greet(dn_row, other)

    own_rows = pl.ds(halo, sub)

    def u_load(ch):
        return pltpu.make_async_copy(u_hbm.at[:, :, lanes_of(col, ch)], u_sc.at[ch, :, my_cols, :], load_sem.at[0, ch])

    def f_load(ch):
        return pltpu.make_async_copy(f_hbm.at[:, :, lanes_of(col, ch)], r_sc.at[ch, own_rows, my_cols, :],
                                     load_sem.at[1, ch])

    mat_load = pltpu.make_async_copy(mat_hbm.at[0, 0], m_raw.at[col], mat_sem)
    kap_load = pltpu.make_async_copy(kap_hbm, k_raw.at[1, col], kap_loc)
    kap_load.start()
    for ch in range(chunks):
        u_load(ch).start()
        f_load(ch).start()
    mat_load.start()

    def u_pair(ch):
        return pltpu.make_async_remote_copy(
            src_ref=u_hbm.at[:, :, lanes_of(other, ch)], dst_ref=u_sc.at[ch, :, my_cols, :],
            send_sem=pair_send.at[0, ch], recv_sem=pair_recv.at[0, ch],
            device_id=(other, row), device_id_type=MESH)

    def u_pair_in(ch):
        return pltpu.make_async_remote_copy(
            src_ref=u_hbm.at[:, :, lanes_of(other, ch)], dst_ref=u_sc.at[ch, :, other_cols, :],
            send_sem=pair_send.at[0, ch], recv_sem=pair_recv.at[0, ch],
            device_id=(other, row), device_id_type=MESH)

    def f_pair(ch, cols):
        return pltpu.make_async_remote_copy(
            src_ref=f_hbm.at[:, :, lanes_of(other, ch)], dst_ref=r_sc.at[ch, own_rows, cols, :],
            send_sem=pair_send.at[1, ch], recv_sem=pair_recv.at[1, ch],
            device_id=(other, row), device_id_type=MESH)

    def mat_pair(slot):
        return pltpu.make_async_remote_copy(
            src_ref=mat_hbm.at[0, 0], dst_ref=m_raw.at[slot],
            send_sem=pair_send.at[2, 0], recv_sem=pair_recv.at[2, 0],
            device_id=(other, row), device_id_type=MESH)

    def kap_copy(band_slot, col_slot, sem_slot, r_to, c_to):
        return pltpu.make_async_remote_copy(
            src_ref=kap_hbm, dst_ref=k_raw.at[band_slot, col_slot],
            send_sem=kap_send.at[sem_slot], recv_sem=kap_recv.at[sem_slot],
            device_id=(c_to, r_to), device_id_type=MESH)

    for ch in range(chunks):
        def clear(i, carry):
            v_sc[ch, i] = jnp.zeros(v_sc.shape[2:], F32)
            return carry
        lax.fori_loop(0, ext + 2, clear, 0)
        e_early[ch, sub - 2:early_rows] = jnp.zeros((early_rows - sub + 2, wide, LANES), BF16)
    omega = om_ref[0]

    pl.semaphore_wait(barrier, 1 + 2 * has_up.astype(jnp.int32) + 2 * has_dn.astype(jnp.int32))

    kap_copy(1, col, 0, row, other).start()
    for ch in range(chunks):
        u_pair(ch).start()
        f_pair(ch, my_cols).start()

    @pl.when(has_up)
    def _():
        kap_copy(2, col, 1, up_row, col).start()
        kap_copy(2, col, 2, up_row, other).start()

    @pl.when(has_dn)
    def _():
        kap_copy(0, col, 3, dn_row, col).start()
        kap_copy(0, col, 4, dn_row, other).start()

    mat_pair(col).start()

    eye = lax.broadcasted_iota(jnp.int32, (sub, sub), 0) == lax.broadcasted_iota(jnp.int32, (sub, sub), 1)

    def spread_row(slot, k_row, at):
        parts = []
        for side in range(2):
            line = k_raw[slot, side, pl.ds(k_row, 1), :]
            picked = jnp.where(eye, jnp.broadcast_to(line, (sub, sub)), 0.0)
            column = jnp.sum(picked, axis=1, keepdims=True)
            parts.append(jnp.broadcast_to(column, (sub, LANES)))
        kb[at, left:left + sub] = parts[0]
        kb[at, left + sub:left + wide] = parts[1]
        kb[at, left - 1:left] = parts[0][0:1]
        kb[at, left + wide:left + wide + 1] = parts[1][sub - 1:sub]

    def side_faces(e):
        k_mid = kb[e + 1, left:left + wide]
        fw[e] = 0.5 * (k_mid + kb[e + 1, left - 1:left + wide - 1])
        fe[e] = 0.5 * (kb[e + 1, left + 1:left + wide + 1] + k_mid)

    def diag_row(e):
        dg[e] = fv[e] + fv[e + 1] + fw[e] + fe[e]

    def face_row(i):
        fv[i] = 0.5 * (kb[i + 1, left:left + wide] + kb[i, left:left + wide])

    kap_load.wait()
    kap_copy(1, other, 0, row, other).wait_recv()

    def own_spread(i, carry):
        spread_row(1, i, i + band)
        return carry
    lax.fori_loop(0, sub, own_spread, 0)

    fv[halo] = jnp.zeros((wide, LANES), F32)
    fv[halo + sub] = jnp.zeros((wide, LANES), F32)

    def own_face(i, carry):
        face_row(i)
        return carry
    lax.fori_loop(halo + 1, halo + sub, own_face, 0)

    def own_side(e, carry):
        side_faces(e)
        diag_row(e)
        return carry
    lax.fori_loop(halo, halo + sub, own_side, 0)

    def stencil(ch, e, n):
        rows = pl.ds(e, n)
        mid = pl.ds(e + 1, n)
        return (dg[rows] * v_sc[ch, mid, left:left + wide]
                - fv[rows] * v_sc[ch, pl.ds(e, n), left:left + wide]
                - fv[mid] * v_sc[ch, pl.ds(e + 2, n), left:left + wide]
                - fw[rows] * v_sc[ch, mid, left - 1:left + wide - 1]
                - fe[rows] * v_sc[ch, mid, left + 1:left + wide + 1])

    def init_copy(way, ch, r_to):
        return pltpu.make_async_remote_copy(
            src_ref=i_send.at[way, ch], dst_ref=i_recv.at[way, ch],
            send_sem=is_sem.at[way, ch], recv_sem=ir_sem.at[way, ch],
            device_id=(col, r_to), device_id_type=MESH)

    def first_residual(ch, carry):
        u_load(ch).wait()
        f_load(ch).wait()
        u_pair_in(ch).wait_recv()
        f_pair(ch, other_cols).wait_recv()

        def fill(i, c):
            v_sc[ch, i + band, left:left + wide] = u_sc[ch, i]
            return c
        lax.fori_loop(0, sub, fill, 0)

        def part(e0, n):
            r_sc[ch, pl.ds(e0, n)] = r_sc[ch, pl.ds(e0, n)] - stencil(ch, e0, n)

        part(halo, halo)
        i_send[0, ch, 0:halo] = r_sc[ch, halo:2 * halo]
        i_send[0, ch, halo] = u_sc[ch, 0]

        @pl.when(has_up)
        def _():
            init_copy(0, ch, up_row).start()
        part(sub, halo)
        i_send[1, ch, 0:halo] = r_sc[ch, sub:sub + halo]
        i_send[1, ch, halo] = u_sc[ch, sub - 1]

        @pl.when(has_dn)
        def _():
            init_copy(1, ch, dn_row).start()

        def middle(i, c):
            part(2 * halo + i * halo, halo)
            return c
        lax.fori_loop(0, (sub - 2 * halo) // halo, middle, 0)

        def to_e(i, c):
            e_early[ch, i] = r_sc[ch, i + band].astype(BF16)
            return c
        lax.fori_loop(0, sub - 2, to_e, 0)
        return carry

    lax.fori_loop(0, chunks, first_residual, 0)

    mat_load.wait()
    mat_pair(other).wait_recv()
    ext_cells = m_raw.shape[2]
    tile = 256
    spot = lax.broadcasted_iota(jnp.int32, (ext_cells, tile), 0)

    def permute(n_tile, carry):
        n_at = n_tile * tile + lax.broadcasted_iota(jnp.int32, (1, tile), 1)
        q = lax.shift_right_logical(n_at, 5)
        j = lax.bitwise_and(n_at, 31)
        line = jnp.where(q < band, q, jnp.where(q < 2 * band, q + (ext - 2 * band), q - band))
        out_at = pl.ds(pl.multiple_of(n_tile * tile, tile), tile)
        for side in range(2):
            ext_col = j + halo - 8 * side
            ok = (q < ext) & (ext_col >= 0) & (ext_col < ext)
            want = jnp.where(ok, line * ext + ext_col, -1)
            pick = jnp.where(spot == want, 1.0, 0.0).astype(BF16)
            moved = jnp.dot(m_raw[side], pick, preferred_element_type=F32)
            m_perm[side, :, out_at] = moved.astype(BF16)
        return carry
    lax.fori_loop(0, m_perm.shape[2] // tile, permute, 0)

    def early_dot(ch):
        for side in range(2):
            operand = e_early[ch, :, 16 * side:16 * side + 32, :].reshape(early_rows * 32, LANES)
            acc[ch, side] = jnp.dot(m_perm[side, :, late_k:late_k + early_rows * 32], operand,
                                    preferred_element_type=F32)

    def first_early(ch, carry):
        early_dot(ch)
        return carry
    lax.fori_loop(0, chunks, first_early, 0)

    @pl.when(has_up)
    def _():
        kap_copy(0, col, 3, row, other).wait_recv()
        kap_copy(0, other, 4, row, other).wait_recv()

        def spread(i, c):
            spread_row(0, sub - band + i, i)
            return c
        lax.fori_loop(0, band, spread, 0)

    @pl.when(jnp.logical_not(has_up))
    def _():
        for i in range(band):
            kb[i] = kb[band]

    @pl.when(has_dn)
    def _():
        kap_copy(2, col, 1, row, other).wait_recv()
        kap_copy(2, other, 2, row, other).wait_recv()

        def spread(i, c):
            spread_row(2, i, band + sub + i)
            return c
        lax.fori_loop(0, band, spread, 0)

    @pl.when(jnp.logical_not(has_dn))
    def _():
        for i in range(band):
            kb[band + sub + i] = kb[band + sub - 1]

    for i in range(halo + 1):
        face_row(i)
        face_row(halo + sub + i)
    for i in range(halo):
        side_faces(i)
        side_faces(halo + sub + i)
    for i in range(halo + 1):
        diag_row(i)
        diag_row(ext - 1 - i)

    def late_e(ch):
        e_late[ch, 0:band] = r_sc[ch, 0:band].astype(BF16)
        e_late[ch, band:2 * band] = r_sc[ch, ext - band:ext].astype(BF16)

    def late_first(ch):
        @pl.when(has_up)
        def _():
            init_copy(1, ch, up_row).wait_recv()
            r_sc[ch, 0:halo] = i_recv[1, ch, 0:halo]

        @pl.when(jnp.logical_not(has_up))
        def _():
            i_recv[1, ch, halo] = jnp.zeros((wide, LANES), F32)
            r_sc[ch, 0:halo] = jnp.zeros((halo, wide, LANES), F32)

        @pl.when(has_dn)
        def _():
            init_copy(0, ch, dn_row).wait_recv()
            r_sc[ch, halo + sub:ext] = i_recv[0, ch, 0:halo]

        @pl.when(jnp.logical_not(has_dn))
        def _():
            i_recv[0, ch, halo] = jnp.zeros((wide, LANES), F32)
            r_sc[ch, halo + sub:ext] = jnp.zeros((halo, wide, LANES), F32)

        flux = fv[halo] * (i_recv[1, ch, halo] - u_sc[ch, 0])
        r_sc[ch, halo - 1] = r_sc[ch, halo - 1] - flux
        r_sc[ch, halo] = r_sc[ch, halo] + flux
        flux = fv[halo + sub] * (i_recv[0, ch, halo] - u_sc[ch, sub - 1])
        r_sc[ch, halo + sub] = r_sc[ch, halo + sub] - flux
        r_sc[ch, halo + sub - 1] = r_sc[ch, halo + sub - 1] + flux
        late_e(ch)

    def z_copy(t, ch, way, r_to):
        return pltpu.make_async_remote_copy(
            src_ref=z_send.at[t, ch, way], dst_ref=z_recv.at[t, ch, way],
            send_sem=zs_sem.at[t, ch, way], recv_sem=zr_sem.at[t, ch, way],
            device_id=(col, r_to), device_id_type=MESH)

    def update(ch, e, n):
        r_new = r_sc[ch, pl.ds(e, n)] - omega * stencil(ch, e, n)
        r_sc[ch, pl.ds(e, n)] = r_new
        return r_new

    def late_next(t, ch):
        @pl.when(has_up)
        def _():
            z_copy(t, ch, 1, up_row).wait_recv()
            v_sc[ch, 0:band, left:left + wide] = z_recv[t, ch, 1].astype(F32)

        @pl.when(has_dn)
        def _():
            z_copy(t, ch, 0, dn_row).wait_recv()
            v_sc[ch, band + sub:band + sub + band, left:left + wide] = z_recv[t, ch, 0].astype(F32)

        e_late[ch, 0:band] = update(ch, 0, band).astype(BF16)
        e_late[ch, band:2 * band] = update(ch, ext - band, band).astype(BF16)

    def late_rows(ch, first, count):
        lo, n = first * sub, count * sub
        sides = []
        for side in range(2):
            operand = e_late[ch, :, 16 * side:16 * side + 32, :].reshape(late_k, LANES)
            part = acc[ch, side, lo:lo + n] + jnp.dot(m_perm[side, lo:lo + n, 0:late_k], operand,
                                                      preferred_element_type=F32)
            sides.append(part.reshape(count, sub, LANES))
        return jnp.concatenate(sides, axis=1).astype(BF16)

    def keep_z(ch, first, count, z_bf):
        v_sc[ch, band + first:band + first + count, left:left + wide] = z_bf.astype(F32)

    def solve_and_send(t, ch):
        z_top = late_rows(ch, 0, band)
        z_bot = late_rows(ch, sub - band, band)
        z_send[t, ch, 0] = z_top
        z_send[t, ch, 1] = z_bot

        @pl.when(has_up)
        def _():
            z_copy(t, ch, 0, up_row).start()

        @pl.when(has_dn)
        def _():
            z_copy(t, ch, 1, dn_row).start()

        keep_z(ch, 0, band, z_top)
        keep_z(ch, sub - band, band, z_bot)
        keep_z(ch, band, sub - 2 * band, late_rows(ch, band, sub - 2 * band))

        group = (sub - 2) // 2

        def inner(i, c):
            e_early[ch, pl.ds(i * group, group)] = update(ch, band + i * group, group).astype(BF16)
            return c
        lax.fori_loop(0, 2, inner, 0)
        add_u(ch)
        early_dot(ch)

    def add_u(ch):
        def add(i, c):
            rows = pl.ds(i * 6, 6)
            u_sc[ch, rows] = u_sc[ch, rows] + omega * v_sc[ch, pl.ds(i * 6 + band, 6), left:left + wide]
            return c
        lax.fori_loop(0, sub // 6, add, 0)

    def sweep_first(ch, carry):
        late_first(ch)
        solve_and_send(0, ch)
        return carry
    lax.fori_loop(0, chunks, sweep_first, 0)

    def sweep_next(step, carry):
        t = step // chunks
        ch = step % chunks
        late_next(t, ch)
        solve_and_send(t + 1, ch)
        return carry
    lax.fori_loop(0, (SWEEPS - 2) * chunks, sweep_next, 0)

    def out_own(ch):
        return pltpu.make_async_copy(u_sc.at[ch, :, my_cols, :], out_hbm.at[:, :, lanes_of(col, ch)], out_loc.at[ch])

    def out_pair(ch, which):
        return pltpu.make_async_remote_copy(
            src_ref=u_sc.at[ch, :, other_cols, :], dst_ref=out_hbm.at[:, :, lanes_of(which, ch)],
            send_sem=out_send.at[ch], recv_sem=out_recv.at[ch],
            device_id=(other, row), device_id_type=MESH)

    def sweep_last(ch, carry):
        late_next(SWEEPS - 2, ch)
        keep_z(ch, 0, sub, late_rows(ch, 0, sub))
        add_u(ch)
        out_pair(ch, col).start()
        out_own(ch).start()
        return carry
    lax.fori_loop(0, chunks, sweep_last, 0)

    kap_copy(1, col, 0, row, other).wait_send()
    mat_pair(col).wait_send()
    for ch in range(chunks):
        u_pair(ch).wait_send()
        f_pair(ch, my_cols).wait_send()

    @pl.when(has_up)
    def _():
        kap_copy(2, col, 1, up_row, col).wait_send()
        kap_copy(2, col, 2, up_row, other).wait_send()
        for ch in range(chunks):
            init_copy(0, ch, up_row).wait_send()
            for t in range(SWEEPS - 1):
                z_copy(t, ch, 0, up_row).wait_send()

    @pl.when(has_dn)
    def _():
        kap_copy(0, col, 3, dn_row, col).wait_send()
        kap_copy(0, col, 4, dn_row, other).wait_send()
        for ch in range(chunks):
            init_copy(1, ch, dn_row).wait_send()
            for t in range(SWEEPS - 1):
                z_copy(t, ch, 1, dn_row).wait_send()

    for ch in range(chunks):
        out_own(ch).wait()
        out_pair(ch, col).wait_send()
        out_pair(ch, other).wait_recv()


def solution(mesh):
    row_count = mesh.shape['row']
    grid_spec = P('row', 'col', None)

    def device_fn(f_blk, u_blk, kappa_blk, mat_blk, omega_relax):
        sub, _, rhs = u_blk.shape
        ext_cells = mat_blk.shape[3]
        ext = math.isqrt(ext_cells)
        halo = (ext - sub) // 2
        band = halo + 1
        chunks = rhs // (2 * LANES)
        wide = 2 * sub
        early_rows = 24
        hbm = pl.BlockSpec(memory_space=pl.ANY)
        dma = pltpu.SemaphoreType.DMA
        return pl.pallas_call(
            functools.partial(kernel, row_count, sub, halo, chunks),
            out_shape=jax.ShapeDtypeStruct(u_blk.shape, F32),
            in_specs=[pl.BlockSpec(memory_space=pltpu.SMEM), hbm, hbm, hbm, hbm],
            out_specs=hbm,
            scratch_shapes=[
                pltpu.VMEM((chunks, sub, wide, LANES), F32),
                pltpu.VMEM((chunks, ext, wide, LANES), F32),
                pltpu.VMEM((chunks, ext + 2, 64, LANES), F32),
                pltpu.VMEM((chunks, 2 * band, wide, LANES), BF16),
                pltpu.VMEM((chunks, early_rows, wide, LANES), BF16),
                pltpu.VMEM((chunks, 2, sub * sub, LANES), F32),
                pltpu.VMEM((2, sub * sub, ext_cells), BF16),
                pltpu.VMEM((2, sub * sub, 1024), BF16),
                pltpu.VMEM((3, 2, sub, sub), F32),
                pltpu.VMEM((ext + 2, 64, LANES), F32),
                pltpu.VMEM((ext + 1, wide, LANES), F32),
                pltpu.VMEM((ext, wide, LANES), F32),
                pltpu.VMEM((ext, wide, LANES), F32),
                pltpu.VMEM((ext, wide, LANES), F32),
                pltpu.VMEM((2, chunks, band, wide, LANES), F32),
                pltpu.VMEM((2, chunks, band, wide, LANES), F32),
                pltpu.VMEM((SWEEPS - 1, chunks, 2, band, wide, LANES), BF16),
                pltpu.VMEM((SWEEPS - 1, chunks, 2, band, wide, LANES), BF16),
                dma((2, chunks)), dma((3, chunks)), dma((3, chunks)), dma, dma, dma((5,)), dma((5,)),
                dma((2, chunks)), dma((2, chunks)),
                dma((SWEEPS - 1, chunks, 2)), dma((SWEEPS - 1, chunks, 2)),
                dma((chunks,)), dma((chunks,)), dma((chunks,)),
            ],
            compiler_params=pltpu.CompilerParams(collective_id=0, has_side_effects=True,
                                                 vmem_limit_bytes=48 * 1024 * 1024),
        )(omega_relax.reshape(1), f_blk, u_blk, kappa_blk, mat_blk)

    return jax.shard_map(device_fn, mesh=mesh,
                         in_specs=(grid_spec, grid_spec, P('row', 'col'), P('row', 'col', None, None), P()),
                         out_specs=grid_spec, check_vma=False)
```

time: 268 us -> 53.5 us (0.20); the launches traced: 265 us -> 53.3 us
  starting transfers between devices: 186 us -> 0 us
  Pallas kernels: 0 us -> 48.6 us
  other arithmetic: 23.9 us -> 0 us
  waiting for transfers between devices: 19.1 us -> 0 us
  local copies, waits for them, and re-layouts: 22.5 us -> 3.87 us
  matrix products: 11 us -> 0 us
    ppermute x52 -> x0, starting transfers between devices: 186 us -> none  [shift_from(): return lax.ppermute(values, axis_name, pair_list)]
    pallas_call x0 -> x1, Pallas kernels: none -> 48.6 us  [device_fn(): pl.pallas_call(functools.partial(kernel, row_count, sub, halo, chunks), o...]
    ppermute x52 -> x0, waiting for transfers between devices: 19.1 us -> none  [shift_from(): return lax.ppermute(values, axis_name, pair_list)]
    convert_element_type x26 -> x0, other arithmetic: 12.5 us -> none  [the longest x6 11.9 us: device_fn(): residual.astype(jnp.bfloat16)]
    slice x32 -> x0, local copies, waits for them, and re-layouts: 12.1 us -> none  [the longest x5 4.43 us: apply_local(): up_nb = jnp.concatenate([from_above, center[:-1]], axis=0)]
    dot_general x6 -> x0, matrix products: 11 us -> none  [device_fn(): jnp.dot(solve_mat, ext_block.reshape(ext_cells, rhs_count), preferred_ele...]
    reshape x6 -> x0, local copies, waits for them, and re-layouts: 10.3 us -> none  [device_fn(): ext_block.reshape(ext_cells, rhs_count)]
    concatenate x6 -> x0, other arithmetic: 7.23 us -> none  [extend_block(): return jnp.concatenate([left_strip, tall_ext, right_strip], axis=1)]
  transfers between devices with their start and end apart: 52 -> 0, of which waited for: 19 -> 0; matrix products, arithmetic and copies ran while one was open for 4% -> 0% of each run, Pallas kernels for 0% -> 0%
where the time goes in v1:
time: 53.5 us; the launch traced here: 53.3 us
  Pallas kernels  48.6 us (91%)
  local copies, waits for them, and re-layouts  3.87 us (7%)
  between operations  0.79 us (1%)
    pallas_call x1, Pallas kernels, device_fn(): pl.pallas_call(functools.partial(kernel, row_count, sub, halo, chunks), o...  48.6 us
    unnamed x8, local copies, waits for them, and re-layouts  3.87 us

profile of v1, /device:TPU:97, one launch (start us, length us, event | category | flops | bytes accessed | tf_op | source)
XLA Modules:
  0.0 53.3 jit_solution(17663749723595455874)
XLA Ops:
  0.0 0.0 copy-start.2
  0.0 0.0 copy-start
  0.8 1.6 %copy.6.mat_hbm = bf16[1,1,576,900]{3,2,1,0:T(8,128)(2,1)S(1)} copy(bf16[1,1,576,900]{2,3,1,0:T(8,128)(2,1)} %param.8) | data formatting | bytes 2073600 | tf_op args[3]
  2.3 0.0 copy-done.2
  2.4 0.0 copy-done
  2.4 0.0 copy-start.1
  2.4 1.3 %copy-done.1 = f32[24,24,512]{2,1,0:T(8,128)S(1)} copy-done((f32[24,24,512]{2,1,0:T(8,128)S(1)}, f32[24,24,512]{2,1,0:T(8,128)}, u32[]{:S(2)}) %copy-start.1) | copy-done | bytes 1179672
  3.6 48.6 %shard_map.55 = f32[24,24,512]{2,1,0:T(8,128)S(1)} custom-call(f32[1]{0:T(128)} %bitcast.1.om_ref, f32[24,24,512]{2,1,0:T(8,128)S(1)} %copy-done, f32[24,24,512]{2,1,0:T(8,128)S(1)} %copy-done.1, f32[24,24]{1,0:T(8,128)S(1)} %copy-done.2, bf16[1,1,576,900]{3,2,1,0:T(8,128)(2,1)S(1)} %copy.6.mat_hbm), custom_call_target="tpu_custom_call" | custom-call | tf_op jit(solution)/shard_map/pallas_call | solution.py:495
  52.3 1.0 %copy.9 = f32[24,24,512]{2,1,0:T(8,128)} copy(f32[24,24,512]{2,1,0:T(8,128)S(1)} %shard_map.55) | data formatting | bytes 2359296
Async XLA Ops:
  0.0 2.3 %copy-start.2 = (f32[24,24]{1,0:T(8,128)S(1)}, f32[24,24]{1,0:T(8,128)}, u32[]{:S(2)}) copy-start(f32[24,24]{1,0:T(8,128)} %kap_hbm.1) | copy-start | bytes 6916
  0.0 2.4 %copy-start = (f32[24,24,512]{2,1,0:T(8,128)S(1)}, f32[24,24,512]{2,1,0:T(8,128)}, u32[]{:S(2)}) copy-start(f32[24,24,512]{2,1,0:T(8,128)} %f_hbm.1) | copy-start | bytes 3538948
  2.4 1.3 %copy-start.1 = (f32[24,24,512]{2,1,0:T(8,128)S(1)}, f32[24,24,512]{2,1,0:T(8,128)}, u32[]{:S(2)}) copy-start(f32[24,24,512]{2,1,0:T(8,128)} %u_hbm.1) | copy-start | bytes 3538948

commit v2 on v0

v2 whole, which is shorter than its diff:
```python
import functools
import math

import jax
import jax.numpy as jnp
from jax import lax
from jax.experimental import pallas as pl
from jax.experimental.pallas import tpu as pltpu
from jax.sharding import PartitionSpec as P

SWEEPS = 6
LANES = 128
MESH = pl.DeviceIdType.MESH
F32 = jnp.float32
BF16 = jnp.bfloat16


def kernel(row_count, sub, halo, chunks,
           om_ref, f_hbm, u_hbm, kap_hbm, mat_hbm, out_ref,
           u_sc, r_sc, v_sc, e_late, e_early, acc, m_raw, m_turn, m_perm,
           k_raw, kb, ko, fv, fw, fe, dg, u_band, pv, pw, pe, pd, i_send, i_recv, a_send, a_recv,
           z_send, z_recv, u_fin,
           load_sem, band_sem, pair_send, pair_recv, mat_sem, kap_loc, kap_send, kap_recv,
           is_sem, ir_sem, as_sem, ar_sem, zs_sem, zr_sem, out_send, out_recv):
    wide = 2 * sub
    ext = sub + 2 * halo
    band = halo + 1
    late_k = 2 * band * 32
    early_rows = e_early.shape[1]
    half = chunks * LANES
    left = 8

    row = lax.axis_index('row')
    col = lax.axis_index('col')
    other = 1 - col
    mine = lax.rem(row + col, 2)
    theirs = 1 - mine
    has_up = row > 0
    has_dn = row < row_count - 1
    ways = ((0, has_up, jnp.maximum(row - 1, 0)), (1, has_dn, jnp.minimum(row + 1, row_count - 1)))
    up_row, dn_row = ways[0][2], ways[1][2]
    col_spans = [pl.ds(side * sub, sub) for side in range(2)]
    my_cols = pl.ds(pl.multiple_of(col * sub, 8), sub)
    other_cols = pl.ds(pl.multiple_of(other * sub, 8), sub)
    own_rows = pl.ds(halo, sub)

    def lanes_of(which, ch):
        return pl.ds(pl.multiple_of(which * half + ch * LANES, LANES), LANES)

    barrier = pltpu.get_barrier_semaphore()

    def greet(r_to, c_to):
        pl.semaphore_signal(barrier, inc=1, device_id=(c_to, r_to), device_id_type=MESH)

    for _, present, r_to in ways:
        @pl.when(present)
        def _():
            greet(r_to, col)
            greet(r_to, other)
    greet(row, other)

    kap_load = pltpu.make_async_copy(kap_hbm, k_raw.at[col], kap_loc)
    kap_load.start()

    def band_loads(way, g):
        lanes = pl.ds(g * LANES, LANES)
        u_from = pl.ds(0 if way == 0 else sub - band, band)
        f_from = pl.ds(0 if way == 0 else sub - halo, halo)
        return (pltpu.make_async_copy(u_hbm.at[u_from, :, lanes], u_band.at[way, g, :, 8:8 + sub, :],
                                      band_sem.at[0, way, g]),
                pltpu.make_async_copy(f_hbm.at[f_from, :, lanes], i_send.at[way, g, 0:halo],
                                      band_sem.at[1, way, g]))

    for g in range(2 * chunks):
        for way in range(2):
            for load in band_loads(way, g):
                load.start()

    def u_load(ch):
        return pltpu.make_async_copy(u_hbm.at[:, :, lanes_of(mine, ch)], u_sc.at[ch, :, my_cols, :], load_sem.at[0, ch])

    def f_load(ch):
        return pltpu.make_async_copy(f_hbm.at[:, :, lanes_of(mine, ch)], r_sc.at[ch, own_rows, my_cols, :],
                                     load_sem.at[1, ch])

    mat_load = pltpu.make_async_copy(mat_hbm, m_raw.at[col], mat_sem)
    mat_load.start()
    for ch in range(chunks):
        u_load(ch).start()
        f_load(ch).start()

    def u_pair(ch, cols):
        return pltpu.make_async_remote_copy(
            src_ref=u_hbm.at[:, :, lanes_of(theirs, ch)], dst_ref=u_sc.at[ch, :, cols, :],
            send_sem=pair_send.at[0, ch], recv_sem=pair_recv.at[0, ch],
            device_id=(other, row), device_id_type=MESH)

    def f_pair(ch, cols):
        return pltpu.make_async_remote_copy(
            src_ref=f_hbm.at[:, :, lanes_of(theirs, ch)], dst_ref=r_sc.at[ch, own_rows, cols, :],
            send_sem=pair_send.at[1, ch], recv_sem=pair_recv.at[1, ch],
            device_id=(other, row), device_id_type=MESH)

    def mat_pair(slot):
        return pltpu.make_async_remote_copy(
            src_ref=mat_hbm, dst_ref=m_raw.at[slot],
            send_sem=pair_send.at[2, 0], recv_sem=pair_recv.at[2, 0],
            device_id=(other, row), device_id_type=MESH)

    def kap_pair(slot):
        return pltpu.make_async_remote_copy(
            src_ref=k_raw.at[col], dst_ref=k_raw.at[slot],
            send_sem=kap_send, recv_sem=kap_recv,
            device_id=(other, row), device_id_type=MESH)

    def core_for(h):
        return lax.rem(h + row + 1, 2)

    def init_send(way, r_to, h, ch):
        g = h * chunks + ch
        return pltpu.make_async_remote_copy(
            src_ref=i_send.at[way, g], dst_ref=i_recv.at[way, ch, :, my_cols, :],
            send_sem=is_sem.at[way, g], recv_sem=ir_sem.at[way, ch, col],
            device_id=(core_for(h), r_to), device_id_type=MESH)

    def init_wait(way, r_to, ch, side):
        pltpu.make_async_remote_copy(
            src_ref=i_send.at[way, ch], dst_ref=i_recv.at[way, ch, :, col_spans[side], :],
            send_sem=is_sem.at[way, ch], recv_sem=ir_sem.at[way, ch, side],
            device_id=(other, r_to), device_id_type=MESH).wait_recv()

    def aux_send(way, r_to, h):
        return pltpu.make_async_remote_copy(
            src_ref=a_send.at[way, h], dst_ref=a_recv.at[way, col],
            send_sem=as_sem.at[way, h], recv_sem=ar_sem.at[way, col],
            device_id=(core_for(h), r_to), device_id_type=MESH)

    def aux_wait(way, r_to, side):
        pltpu.make_async_remote_copy(
            src_ref=a_send.at[way, side], dst_ref=a_recv.at[way, side],
            send_sem=as_sem.at[way, side], recv_sem=ar_sem.at[way, side],
            device_id=(other, r_to), device_id_type=MESH).wait_recv()

    def z_copy(t, ch, way, r_to):
        return pltpu.make_async_remote_copy(
            src_ref=z_send.at[t, ch, way], dst_ref=z_recv.at[t, ch, way],
            send_sem=zs_sem.at[t, ch, way], recv_sem=zr_sem.at[t, ch, way],
            device_id=(other, r_to), device_id_type=MESH)

    omega = om_ref[0]
    for way in range(2):
        for g in range(2 * chunks):
            u_band[way, g, :, 0:8] = jnp.zeros((band, 8, LANES), F32)
            u_band[way, g, :, 8 + sub:16 + sub] = jnp.zeros((band, 8, LANES), F32)
        for h in range(2):
            a_send[way, h] = jnp.zeros((16, LANES), F32)

    eye = lax.broadcasted_iota(jnp.int32, (sub, sub), 0) == lax.broadcasted_iota(jnp.int32, (sub, sub), 1)

    def spread(line):
        picked = jnp.where(eye, jnp.broadcast_to(line, (sub, sub)), 0.0)
        return jnp.broadcast_to(jnp.sum(picked, axis=1, keepdims=True), (sub, LANES))

    kap_load.wait()
    for k in range(sub):
        line = spread(k_raw[col, k:k + 1, :])
        ko[k, 8:8 + sub] = line
        ko[k, 7:8] = line[0:1]
        ko[k, 8 + sub:9 + sub] = line[sub - 1:sub]
    spot_col = lax.broadcasted_iota(jnp.int32, (sub, LANES), 0)
    cut_w = (spot_col == 0) & (col == 1)
    cut_e = (spot_col == sub - 1) & (col == 0)
    for way in range(2):
        first = 0 if way == 0 else sub - halo
        for k in range(halo):
            at = first + k
            mid = ko[at, 8:8 + sub]
            pw[way, k] = jnp.where(cut_w, 0.0, 0.5 * (mid + ko[at, 7:7 + sub]))
            pe[way, k] = jnp.where(cut_e, 0.0, 0.5 * (ko[at, 9:9 + sub] + mid))
            total = pw[way, k] + pe[way, k]
            if at > 0:
                pv[way, k] = 0.5 * (mid + ko[at - 1, 8:8 + sub])
                total = total + pv[way, k]
            if at < sub - 1:
                pv[way, k + 1] = 0.5 * (ko[at + 1, 8:8 + sub] + mid)
                total = total + pv[way, k + 1]
            pd[way, k] = total

    for g in range(2 * chunks):
        for way in range(2):
            for load in band_loads(way, g):
                load.wait()
            shift = 0 if way == 0 else 1
            for k in range(halo):
                line = shift + k
                au = (pd[way, k] * u_band[way, g, line, 8:8 + sub]
                      - pw[way, k] * u_band[way, g, line, 7:7 + sub]
                      - pe[way, k] * u_band[way, g, line, 9:9 + sub])
                if line > 0:
                    au = au - pv[way, k] * u_band[way, g, line - 1, 8:8 + sub]
                if line < band - 1:
                    au = au - pv[way, k + 1] * u_band[way, g, line + 1, 8:8 + sub]
                i_send[way, g, k] = i_send[way, g, k] - au
                edge = jnp.where(col == 0, u_band[way, g, line, 7 + sub:8 + sub], u_band[way, g, line, 8:9])
                slot = halo * (g % chunks) + k
                a_send[way, g // chunks, slot:slot + 1] = edge
            i_send[way, g, halo] = u_band[way, g, 0 if way == 0 else halo, 8:8 + sub]

        for h in range(2):
            if g == 0:
                a_send[0, h, 8:8 + band, 0:sub] = k_raw[col, 0:band]
                a_send[1, h, 8:8 + band, 0:sub] = k_raw[col, sub - band:sub]

    pl.semaphore_wait(barrier, 1 + 2 * has_up.astype(jnp.int32) + 2 * has_dn.astype(jnp.int32))

    for way, present, r_to in ways:
        @pl.when(present)
        def _():
            for h in range(2):
                aux_send(way, r_to, h).start()
            for ch in range(chunks):
                for h in range(2):
                    init_send(way, r_to, h, ch).start()
    kap_pair(col).start()
    u_pair(0, my_cols).start()
    f_pair(0, my_cols).start()
    mat_pair(col).start()
    for ch in range(1, chunks):
        u_pair(ch, my_cols).start()
        f_pair(ch, my_cols).start()

    def clear(ch, carry):
        for i in list(range(band)) + list(range(band + sub, ext + 2)):
            v_sc[ch, i] = jnp.zeros(v_sc.shape[2:], F32)
        for i in range(band, band + sub):
            v_sc[ch, i, 0:8] = jnp.zeros((8, LANES), F32)
            v_sc[ch, i, 8 + wide:16 + wide] = jnp.zeros((8, LANES), F32)
        e_early[ch, sub - 2:early_rows] = jnp.zeros((early_rows - sub + 2, wide, LANES), BF16)
        return carry
    lax.fori_loop(0, chunks, clear, 0)

    ext_cells = m_raw.shape[1]
    tile = 256
    lines_per_tile = tile // 32

    def permute(side):
        m_turn[:, 896:1024] = jnp.zeros((sub * sub, 128), BF16)
        m_turn[:, 0:ext_cells] = m_raw[side].T
        for n_tile in range(m_perm.shape[2] // tile):
            if n_tile == 0:
                spans = [(0, 128), (768, 1024)]
            else:
                first = band + lines_per_tile * (n_tile - 1)
                last = min(first + lines_per_tile, ext - band)
                spans = [(first * ext // 128 * 128, -(-last * ext // 128) * 128)]
            n_at = n_tile * tile + lax.broadcasted_iota(jnp.int32, (1, tile), 1)
            q = lax.shift_right_logical(n_at, 5)
            j = lax.bitwise_and(n_at, 31)
            line = jnp.where(q < band, q, jnp.where(q < 2 * band, q + (ext - 2 * band), q - band))
            ext_col = j + (halo - 8 * side)
            ok = (q < ext) & (ext_col >= 0) & (ext_col < ext)
            want = jnp.where(ok, line * ext + ext_col, -1)
            moved = None
            for lo, hi in spans:
                spot = lo + lax.broadcasted_iota(jnp.int32, (hi - lo, tile), 0)
                pick = jnp.where(spot == want, 1.0, 0.0).astype(BF16)
                part = jnp.dot(m_turn[:, lo:hi], pick, preferred_element_type=F32)
                moved = part if moved is None else moved + part
            m_perm[side, :, n_tile * tile:(n_tile + 1) * tile] = moved.astype(BF16)

    mat_load.wait()
    permute(col)

    kap_pair(other).wait_recv()

    def put_rows(take, at, count):
        for k in range(count):
            for side in range(2):
                line = spread(take(side, k))
                kb[at + k, left + side * sub:left + (side + 1) * sub] = line
                if side == 0:
                    kb[at + k, left - 1:left] = line[0:1]
                else:
                    kb[at + k, left + wide:left + wide + 1] = line[sub - 1:sub]

    def side_faces(e):
        k_mid = kb[e + 1, left:left + wide]
        fw[e] = 0.5 * (k_mid + kb[e + 1, left - 1:left + wide - 1])
        fe[e] = 0.5 * (kb[e + 1, left + 1:left + wide + 1] + k_mid)

    def diag_row(e):
        dg[e] = fv[e] + fv[e + 1] + fw[e] + fe[e]

    def face_row(i):
        fv[i] = 0.5 * (kb[i + 1, left:left + wide] + kb[i, left:left + wide])

    put_rows(lambda side, k: k_raw[side, k:k + 1, :], band, sub)
    fv[halo] = jnp.zeros((wide, LANES), F32)
    fv[halo + sub] = jnp.zeros((wide, LANES), F32)

    def own_face(i, carry):
        face_row(i)
        return carry
    lax.fori_loop(halo + 1, halo + sub, own_face, 0)

    def own_side(e, carry):
        side_faces(e)
        diag_row(e)
        return carry
    lax.fori_loop(halo, halo + sub, own_side, 0)

    def stencil(ch, e, n):
        rows = pl.ds(e, n)
        mid = pl.ds(e + 1, n)
        return (dg[rows] * v_sc[ch, mid, left:left + wide]
                - fv[rows] * v_sc[ch, pl.ds(e, n), left:left + wide]
                - fv[mid] * v_sc[ch, pl.ds(e + 2, n), left:left + wide]
                - fw[rows] * v_sc[ch, mid, left - 1:left + wide - 1]
                - fe[rows] * v_sc[ch, mid, left + 1:left + wide + 1])

    def first_residual(ch):
        u_load(ch).wait()
        f_load(ch).wait()
        u_pair(ch, other_cols).wait_recv()
        f_pair(ch, other_cols).wait_recv()

        def fill(i, c):
            rows = pl.ds(i * 6, 6)
            v_sc[ch, pl.ds(i * 6 + band, 6), left:left + wide] = u_sc[ch, rows]
            return c
        lax.fori_loop(0, sub // 6, fill, 0)

        def part(i, c):
            rows = pl.ds(halo + i * 6, 6)
            r_sc[ch, rows] = r_sc[ch, rows] - stencil(ch, halo + i * 6, 6)
            return c
        lax.fori_loop(0, sub // 6, part, 0)
        group = (sub - 2) // 2

        def to_e(i, c):
            e_early[ch, pl.ds(i * group, group)] = r_sc[ch, pl.ds(i * group + band, group)].astype(BF16)
            return c
        lax.fori_loop(0, 2, to_e, 0)

    first_residual(0)

    mat_pair(other).wait_recv()
    permute(other)

    def early_dot(ch):
        for side in range(2):
            operand = e_early[ch, :, 16 * side:16 * side + 32, :].reshape(early_rows * 32, LANES)
            acc[ch, side] = jnp.dot(m_perm[side, :, late_k:late_k + early_rows * 32], operand,
                                    preferred_element_type=F32)

    for way, present, r_to in ways:
        @pl.when(present)
        def _():
            for side in range(2):
                aux_wait(1 - way, r_to, side)
            put_rows(lambda side, k: a_recv[1 - way, side, 8 + k:9 + k, 0:sub], 0 if way == 0 else band + sub, band)

        @pl.when(jnp.logical_not(present))
        def _():
            for side in range(2):
                a_recv[1 - way, side] = jnp.zeros((16, LANES), F32)
            for i in range(band):
                if way == 0:
                    kb[i] = kb[band]
                else:
                    kb[band + sub + i] = kb[band + sub - 1]

    for i in range(halo + 1):
        face_row(i)
        face_row(halo + sub + i)
    for i in range(halo):
        side_faces(i)
        side_faces(halo + sub + i)
    for i in range(halo + 1):
        diag_row(i)
        diag_row(ext - 1 - i)

    def late_first(ch):
        for way, present, r_to in ways:
            sent = 1 - way
            rows = pl.ds(0 if way == 0 else halo + sub, halo)

            @pl.when(present)
            def _():
                for side in range(2):
                    init_wait(sent, r_to, ch, side)
                r_sc[ch, rows] = i_recv[sent, ch, 0:halo]

            @pl.when(jnp.logical_not(present))
            def _():
                i_recv[sent, ch, halo] = jnp.zeros((wide, LANES), F32)
                r_sc[ch, rows] = jnp.zeros((halo, wide, LANES), F32)

            for k in range(halo):
                e = (0 if way == 0 else halo + sub) + k
                slot = pl.ds(halo * ch + k, 1)
                flux = fe[e, sub - 1:sub] * (a_recv[sent, 1, slot] - a_recv[sent, 0, slot])
                r_sc[ch, e, sub - 1:sub] = r_sc[ch, e, sub - 1:sub] + flux
                r_sc[ch, e, sub:sub + 1] = r_sc[ch, e, sub:sub + 1] - flux

        closed = jnp.where(ch > 0, 1.0, 0.0)
        flux = fv[halo] * (i_recv[1, ch, halo] - u_sc[ch, 0])
        r_sc[ch, halo - 1] = r_sc[ch, halo - 1] - flux
        r_sc[ch, halo] = r_sc[ch, halo] + (flux + closed * (fv[halo] * u_sc[ch, 0]))
        flux = fv[halo + sub] * (i_recv[0, ch, halo] - u_sc[ch, sub - 1])
        r_sc[ch, halo + sub] = r_sc[ch, halo + sub] - flux
        last = halo + sub - 1
        r_sc[ch, last] = r_sc[ch, last] + (flux + closed * (fv[halo + sub] * u_sc[ch, sub - 1]))
        e_late[ch, 0:band] = r_sc[ch, 0:band].astype(BF16)
        e_late[ch, band:2 * band] = r_sc[ch, ext - band:ext].astype(BF16)

    def update(ch, e, n):
        r_new = r_sc[ch, pl.ds(e, n)] - omega * stencil(ch, e, n)
        r_sc[ch, pl.ds(e, n)] = r_new
        return r_new

    def late_next(t, ch):
        for way, present, r_to in ways:
            @pl.when(present)
            def _():
                z_copy(t, ch, 1 - way, r_to).wait_recv()
                at = 0 if way == 0 else band + sub
                v_sc[ch, at:at + band, left:left + wide] = z_recv[t, ch, 1 - way].astype(F32)

        e_late[ch, 0:band] = update(ch, 0, band).astype(BF16)
        e_late[ch, band:2 * band] = update(ch, ext - band, band).astype(BF16)

    def solve(ch, side, first, count):
        lo, n = first * sub, count * sub
        cols = pl.ds(pl.multiple_of(16 * side, 16), 32)
        operand = e_late[ch, :, cols, :].reshape(late_k, LANES)
        part = acc[ch, side, lo:lo + n] + jnp.dot(m_perm[side, lo:lo + n, 0:late_k], operand,
                                                  preferred_element_type=F32)
        return part.reshape(count, sub, LANES)

    def solve_rows(ch, first, count):
        return jnp.concatenate([solve(ch, side, first, count) for side in range(2)], axis=1).astype(BF16)

    def keep_z(ch, first, count, z_bf):
        v_sc[ch, band + first:band + first + count, left:left + wide] = z_bf.astype(F32)

    def solve_and_send(t, ch):
        z_top = solve_rows(ch, 0, band)
        z_bot = solve_rows(ch, sub - band, band)
        z_send[t, ch, 0] = z_top
        z_send[t, ch, 1] = z_bot
        for way, present, r_to in ways:
            @pl.when(present)
            def _():
                z_copy(t, ch, way, r_to).start()

        keep_z(ch, 0, band, z_top)
        keep_z(ch, sub - band, band, z_bot)
        keep_z(ch, band, sub - 2 * band, solve_rows(ch, band, sub - 2 * band))

        group = (sub - 2) // 2

        def inner(i, c):
            e_early[ch, pl.ds(i * group, group)] = update(ch, band + i * group, group).astype(BF16)
            return c
        lax.fori_loop(0, 2, inner, 0)

        def add(i, c):
            rows = pl.ds(i * 6, 6)
            u_sc[ch, rows] = u_sc[ch, rows] + omega * v_sc[ch, pl.ds(i * 6 + band, 6), left:left + wide]
            return c
        lax.fori_loop(0, sub // 6, add, 0)
        early_dot(ch)

    def sweep_first(ch, carry):
        @pl.when(ch > 0)
        def _():
            first_residual(ch)
        early_dot(ch)
        late_first(ch)
        solve_and_send(0, ch)
        return carry
    lax.fori_loop(0, chunks, sweep_first, 0)

    def sweep_next(step, carry):
        t = step // chunks
        ch = step % chunks
        late_next(t, ch)
        solve_and_send(t + 1, ch)
        return carry
    lax.fori_loop(0, (SWEEPS - 2) * chunks, sweep_next, 0)

    pieces = 2
    piece = sub // pieces

    def out_pair(ch, n, which):
        rows = pl.ds(n * piece, piece)
        return pltpu.make_async_remote_copy(
            src_ref=u_fin.at[ch, rows], dst_ref=out_ref.at[rows, :, lanes_of(which, ch)],
            send_sem=out_send.at[ch, n], recv_sem=out_recv.at[ch, n],
            device_id=(other, row), device_id_type=MESH)

    def sweep_last(ch, carry):
        late_next(SWEEPS - 2, ch)
        for n in range(pieces):
            first = n * piece
            z = solve(ch, other, first, piece).astype(BF16).astype(F32)
            u_fin[ch, first:first + piece] = u_sc[ch, first:first + piece, other_cols] + omega * z
            out_pair(ch, n, mine).start()
        for n in range(pieces):
            first = n * piece
            z = solve(ch, col, first, piece).astype(BF16).astype(F32)
            out_ref[first:first + piece, :, lanes_of(mine, ch)] = u_sc[ch, first:first + piece, my_cols] + omega * z
        return carry
    lax.fori_loop(0, chunks, sweep_last, 0)

    kap_pair(col).wait_send()
    mat_pair(col).wait_send()
    for ch in range(chunks):
        u_pair(ch, my_cols).wait_send()
        f_pair(ch, my_cols).wait_send()
    for way, present, r_to in ways:
        @pl.when(present)
        def _():
            for h in range(2):
                aux_send(way, r_to, h).wait_send()
                for ch in range(chunks):
                    init_send(way, r_to, h, ch).wait_send()
            for ch in range(chunks):
                for t in range(SWEEPS - 1):
                    z_copy(t, ch, way, r_to).wait_send()
    for ch in range(chunks):
        for n in range(pieces):
            out_pair(ch, n, mine).wait_send()
            out_pair(ch, n, theirs).wait_recv()


def solution(mesh):
    row_count = mesh.shape['row']
    grid_spec = P('row', 'col', None)

    def device_fn(f_blk, u_blk, kappa_blk, mat_blk, omega_relax):
        sub, _, rhs = u_blk.shape
        ext_cells = mat_blk.shape[3]
        ext = math.isqrt(ext_cells)
        halo = (ext - sub) // 2
        band = halo + 1
        chunks = rhs // (2 * LANES)
        wide = 2 * sub
        early_rows = 24
        hbm = pl.BlockSpec(memory_space=pl.ANY)
        vmem = pltpu.VMEM
        dma = pltpu.SemaphoreType.DMA
        return pl.pallas_call(
            functools.partial(kernel, row_count, sub, halo, chunks),
            out_shape=pltpu.VMEM(u_blk.shape, F32),
            in_specs=[pl.BlockSpec(memory_space=pltpu.SMEM), hbm, hbm, hbm, hbm],
            out_specs=pl.BlockSpec(memory_space=pltpu.VMEM),
            scratch_shapes=[
                vmem((chunks, sub, wide, LANES), F32),
                vmem((chunks, ext, wide, LANES), F32),
                vmem((chunks, ext + 2, 64, LANES), F32),
                vmem((chunks, 2 * band, wide, LANES), BF16),
                vmem((chunks, early_rows, wide, LANES), BF16),
                vmem((chunks, 2, sub * sub, LANES), F32),
                vmem((2, ext_cells, sub * sub), BF16),
                vmem((sub * sub, 1024), BF16),
                vmem((2, sub * sub, 1024), BF16),
                vmem((2, sub, sub), F32),
                vmem((ext + 2, 64, LANES), F32),
                vmem((sub, 40, LANES), F32),
                vmem((ext + 1, wide, LANES), F32),
                vmem((ext, wide, LANES), F32),
                vmem((ext, wide, LANES), F32),
                vmem((ext, wide, LANES), F32),
                vmem((2, 2 * chunks, band, 40, LANES), F32),
                vmem((2, halo + 1, sub, LANES), F32),
                vmem((2, halo, sub, LANES), F32),
                vmem((2, halo, sub, LANES), F32),
                vmem((2, halo, sub, LANES), F32),
                vmem((2, 2 * chunks, band, sub, LANES), F32),
                vmem((2, chunks, band, wide, LANES), F32),
                vmem((2, 2, 16, LANES), F32),
                vmem((2, 2, 16, LANES), F32),
                vmem((SWEEPS - 1, chunks, 2, band, wide, LANES), BF16),
                vmem((SWEEPS - 1, chunks, 2, band, wide, LANES), BF16),
                vmem((chunks, sub, sub, LANES), F32),
                dma((2, chunks)), dma((2, 2, 2 * chunks)), dma((3, chunks)), dma((3, chunks)), dma, dma,
                dma, dma,
                dma((2, 2 * chunks)), dma((2, chunks, 2)), dma((2, 2)), dma((2, 2)),
                dma((SWEEPS - 1, chunks, 2)), dma((SWEEPS - 1, chunks, 2)),
                dma((chunks, 2)), dma((chunks, 2)),
            ],
            compiler_params=pltpu.CompilerParams(collective_id=0, has_side_effects=True,
                                                 vmem_limit_bytes=61000 * 1024),
        )(omega_relax.reshape(1), f_blk, u_blk, kappa_blk, mat_blk[0, 0].T)

    return jax.shard_map(device_fn, mesh=mesh,
                         in_specs=(grid_spec, grid_spec, P('row', 'col'), P('row', 'col', None, None), P()),
                         out_specs=grid_spec, check_vma=False)
```

time: 268 us -> 45.1 us (0.17); the launches traced: 265 us -> 44.9 us
  starting transfers between devices: 186 us -> 0 us
  Pallas kernels: 0 us -> 43.2 us
  other arithmetic: 23.9 us -> 0 us
  local copies, waits for them, and re-layouts: 22.5 us -> 1.02 us
  waiting for transfers between devices: 19.1 us -> 0 us
  matrix products: 11 us -> 0 us
    ppermute x52 -> x0, starting transfers between devices: 186 us -> none  [shift_from(): return lax.ppermute(values, axis_name, pair_list)]
    pallas_call x0 -> x1, Pallas kernels: none -> 43.2 us  [device_fn(): pl.pallas_call(functools.partial(kernel, row_count, sub, halo, chunks), o...]
    ppermute x52 -> x0, waiting for transfers between devices: 19.1 us -> none  [shift_from(): return lax.ppermute(values, axis_name, pair_list)]
    convert_element_type x26 -> x0, other arithmetic: 12.5 us -> none  [the longest x6 11.9 us: device_fn(): residual.astype(jnp.bfloat16)]
    slice x32 -> x0, local copies, waits for them, and re-layouts: 12.1 us -> none  [the longest x5 4.43 us: apply_local(): up_nb = jnp.concatenate([from_above, center[:-1]], axis=0)]
    dot_general x6 -> x0, matrix products: 11 us -> none  [device_fn(): jnp.dot(solve_mat, ext_block.reshape(ext_cells, rhs_count), preferred_ele...]
    reshape x6 -> x0, local copies, waits for them, and re-layouts: 10.3 us -> none  [device_fn(): ext_block.reshape(ext_cells, rhs_count)]
    concatenate x6 -> x0, other arithmetic: 7.23 us -> none  [extend_block(): return jnp.concatenate([left_strip, tall_ext, right_strip], axis=1)]
  transfers between devices with their start and end apart: 52 -> 0, of which waited for: 19 -> 0; matrix products, arithmetic and copies ran while one was open for 4% -> 0% of each run, Pallas kernels for 0% -> 0%
where the time goes in v2:
time: 45.1 us; the launch traced here: 44.9 us
  Pallas kernels  43.2 us (96%)
  local copies, waits for them, and re-layouts  1.02 us (2%)
  between operations  0.66 us (1%)
    pallas_call x1, Pallas kernels, device_fn(): pl.pallas_call(functools.partial(kernel, row_count, sub, halo, chunks), o...  43.2 us
    unnamed x1, local copies, waits for them, and re-layouts  1.02 us

profile of v2, /device:TPU:97, one launch (start us, length us, event | category | flops | bytes accessed | tf_op | source)
XLA Modules:
  0.0 44.9 jit_solution(12762550774336040258)
XLA Ops:
  0.7 43.2 %shard_map.55 = f32[24,24,512]{2,1,0:T(8,128)S(1)} custom-call(f32[1]{0:T(128)} %bitcast.4.om_ref, f32[24,24,512]{2,1,0:T(8,128)} %f_hbm.1, f32[24,24,512]{2,1,0:T(8,128)} %u_hbm.1, f32[24,24]{1,0:T(8,128)} %kap_hbm.1, bf16[900,576]{1,0:T(8,128)(2,1)} %bitcast.5), custom_call_target="tpu_custom_call" | custom-call | tf_op jit(solution)/shard_map/pallas_call | solution.py:554
  43.9 1.0 %copy.7 = f32[24,24,512]{2,1,0:T(8,128)} copy(f32[24,24,512]{2,1,0:T(8,128)S(1)} %shard_map.55) | data formatting | bytes 2359296

commit v3 on v2

--- a/solution.py
+++ b/solution.py
@@ -18,15 +18,15 @@
 def kernel(row_count, sub, halo, chunks,
            om_ref, f_hbm, u_hbm, kap_hbm, mat_hbm, out_ref,
            u_sc, r_sc, v_sc, e_late, e_early, acc, m_raw, m_turn, m_perm,
-           k_raw, kb, ko, fv, fw, fe, dg, u_band, pv, pw, pe, pd, i_send, i_recv, a_send, a_recv,
+           k_raw, kb, ko, fv, fw, fe, dg, u_band, pv, pw, pe, pd, i_send, i_recv, n_send, n_recv, a_send, a_recv,
            z_send, z_recv, u_fin,
-           load_sem, band_sem, pair_send, pair_recv, mat_sem, kap_loc, kap_send, kap_recv,
-           is_sem, ir_sem, as_sem, ar_sem, zs_sem, zr_sem, out_send, out_recv):
+           load_sem, band_sem, pair_send, pair_recv, mat_sem, mat_send, mat_recv, kap_loc, kap_send, kap_recv,
+           is_sem, ns_sem, ir_sem, far_sem, as_sem, ar_sem, zs_sem, zr_sem, out_send, out_recv):
     wide = 2 * sub
     ext = sub + 2 * halo
     band = halo + 1
     late_k = 2 * band * 32
-    early_rows = e_early.shape[1]
+    early_rows = e_early.shape[0]
     half = chunks * LANES
     left = 8
 
@@ -47,7 +47,17 @@
     def lanes_of(which, ch):
         return pl.ds(pl.multiple_of(which * half + ch * LANES, LANES), LANES)
 
+    def local_bytes(ref, sem):
+        return pltpu.make_async_copy(ref, ref, sem)
+
+    def remote_bytes(ref, send_sem, recv_sem):
+        return pltpu.make_async_remote_copy(src_ref=ref, dst_ref=ref, send_sem=send_sem, recv_sem=recv_sem,
+                                            device_id=(other, row), device_id_type=MESH)
+
     barrier = pltpu.get_barrier_semaphore()
+
+    def in_lanes(ch):
+        return slice(ch * LANES, (ch + 1) * LANES)
 
     def greet(r_to, c_to):
         pl.semaphore_signal(barrier, inc=1, device_id=(c_to, r_to), device_id_type=MESH)
@@ -67,9 +77,9 @@
         u_from = pl.ds(0 if way == 0 else sub - band, band)
         f_from = pl.ds(0 if way == 0 else sub - halo, halo)
         return (pltpu.make_async_copy(u_hbm.at[u_from, :, lanes], u_band.at[way, g, :, 8:8 + sub, :],
-                                      band_sem.at[0, way, g]),
-                pltpu.make_async_copy(f_hbm.at[f_from, :, lanes], i_send.at[way, g, 0:halo],
-                                      band_sem.at[1, way, g]))
+                                      band_sem.at[0]),
+                pltpu.make_async_copy(f_hbm.at[f_from, :, lanes], i_send.at[way, g, pl.ds(1 - way, halo)],
+                                      band_sem.at[1]))
 
     for g in range(2 * chunks):
         for way in range(2):
@@ -77,11 +87,11 @@
                 load.start()
 
     def u_load(ch):
-        return pltpu.make_async_copy(u_hbm.at[:, :, lanes_of(mine, ch)], u_sc.at[ch, :, my_cols, :], load_sem.at[0, ch])
+        return pltpu.make_async_copy(u_hbm.at[:, :, lanes_of(mine, ch)], u_sc.at[ch, :, my_cols, :], load_sem.at[ch])
 
     def f_load(ch):
         return pltpu.make_async_copy(f_hbm.at[:, :, lanes_of(mine, ch)], r_sc.at[ch, own_rows, my_cols, :],
-                                     load_sem.at[1, ch])
+                                     load_sem.at[ch])
 
     mat_load = pltpu.make_async_copy(mat_hbm, m_raw.at[col], mat_sem)
     mat_load.start()
@@ -92,19 +102,19 @@
     def u_pair(ch, cols):
         return pltpu.make_async_remote_copy(
             src_ref=u_hbm.at[:, :, lanes_of(theirs, ch)], dst_ref=u_sc.at[ch, :, cols, :],
-            send_sem=pair_send.at[0, ch], recv_sem=pair_recv.at[0, ch],
+            send_sem=pair_send, recv_sem=pair_recv.at[ch],
             device_id=(other, row), device_id_type=MESH)
 
     def f_pair(ch, cols):
         return pltpu.make_async_remote_copy(
             src_ref=f_hbm.at[:, :, lanes_of(theirs, ch)], dst_ref=r_sc.at[ch, own_rows, cols, :],
-            send_sem=pair_send.at[1, ch], recv_sem=pair_recv.at[1, ch],
+            send_sem=pair_send, recv_sem=pair_recv.at[ch],
             device_id=(other, row), device_id_type=MESH)
 
     def mat_pair(slot):
         return pltpu.make_async_remote_copy(
             src_ref=mat_hbm, dst_ref=m_raw.at[slot],
-            send_sem=pair_send.at[2, 0], recv_sem=pair_recv.at[2, 0],
+            send_sem=mat_send, recv_sem=mat_recv,
             device_id=(other, row), device_id_type=MESH)
 
     def kap_pair(slot):
@@ -116,35 +126,32 @@
     def core_for(h):
         return lax.rem(h + row + 1, 2)
 
-    def init_send(way, r_to, h, ch):
+    near_rows = (pl.ds(0, 2), pl.ds(2, 2))
+    far_rows = (pl.ds(2, 2), pl.ds(0, 2))
+
+    def init_send(way, r_to, h, ch, rows, recv_sem):
         g = h * chunks + ch
         return pltpu.make_async_remote_copy(
-            src_ref=i_send.at[way, g], dst_ref=i_recv.at[way, ch, :, my_cols, :],
-            send_sem=is_sem.at[way, g], recv_sem=ir_sem.at[way, ch, col],
+            src_ref=i_send.at[way, g, rows], dst_ref=i_recv.at[way, ch, rows, my_cols, :],
+            send_sem=is_sem.at[way], recv_sem=recv_sem.at[way, ch],
             device_id=(core_for(h), r_to), device_id_type=MESH)
 
-    def init_wait(way, r_to, ch, side):
-        pltpu.make_async_remote_copy(
-            src_ref=i_send.at[way, ch], dst_ref=i_recv.at[way, ch, :, col_spans[side], :],
-            send_sem=is_sem.at[way, ch], recv_sem=ir_sem.at[way, ch, side],
-            device_id=(other, r_to), device_id_type=MESH).wait_recv()
+    def narrow_send(way, r_to, h, ch):
+        return pltpu.make_async_remote_copy(
+            src_ref=n_send.at[way, h * chunks + ch], dst_ref=n_recv.at[way, ch, col],
+            send_sem=ns_sem.at[way], recv_sem=ir_sem.at[way, ch],
+            device_id=(core_for(h), r_to), device_id_type=MESH)
 
     def aux_send(way, r_to, h):
         return pltpu.make_async_remote_copy(
             src_ref=a_send.at[way, h], dst_ref=a_recv.at[way, col],
-            send_sem=as_sem.at[way, h], recv_sem=ar_sem.at[way, col],
+            send_sem=as_sem.at[way], recv_sem=ar_sem.at[way],
             device_id=(core_for(h), r_to), device_id_type=MESH)
 
-    def aux_wait(way, r_to, side):
-        pltpu.make_async_remote_copy(
-            src_ref=a_send.at[way, side], dst_ref=a_recv.at[way, side],
-            send_sem=as_sem.at[way, side], recv_sem=ar_sem.at[way, side],
-            device_id=(other, r_to), device_id_type=MESH).wait_recv()
-
     def z_copy(t, ch, way, r_to):
         return pltpu.make_async_remote_copy(
-            src_ref=z_send.at[t, ch, way], dst_ref=z_recv.at[t, ch, way],
-            send_sem=zs_sem.at[t, ch, way], recv_sem=zr_sem.at[t, ch, way],
+            src_ref=z_send.at[way, t, ch], dst_ref=z_recv.at[way, t, ch],
+            send_sem=zs_sem.at[way], recv_sem=zr_sem.at[t % 2, ch, way],
             device_id=(other, r_to), device_id_type=MESH)
 
     omega = om_ref[0]
@@ -186,13 +193,19 @@
                 total = total + pv[way, k + 1]
             pd[way, k] = total
 
+    local_bytes(i_send, band_sem.at[0]).wait()
+    local_bytes(i_send.at[:, :, 0:halo], band_sem.at[1]).wait()
+    for way in range(2):
+        for h in range(2):
+            first = 0 if way == 0 else sub - band
+            a_send[way, h, 12:12 + band, 0:sub] = k_raw[col, first:first + band]
     for g in range(2 * chunks):
+        h, ch = g // chunks, g % chunks
         for way in range(2):
-            for load in band_loads(way, g):
-                load.wait()
-            shift = 0 if way == 0 else 1
+            shift = way
             for k in range(halo):
                 line = shift + k
+                at = k + 1 - way
                 au = (pd[way, k] * u_band[way, g, line, 8:8 + sub]
                       - pw[way, k] * u_band[way, g, line, 7:7 + sub]
                       - pe[way, k] * u_band[way, g, line, 9:9 + sub])
@@ -200,16 +213,17 @@
                     au = au - pv[way, k] * u_band[way, g, line - 1, 8:8 + sub]
                 if line < band - 1:
                     au = au - pv[way, k + 1] * u_band[way, g, line + 1, 8:8 + sub]
-                i_send[way, g, k] = i_send[way, g, k] - au
+                part = i_send[way, g, at] - au
+                i_send[way, g, at] = part
                 edge = jnp.where(col == 0, u_band[way, g, line, 7 + sub:8 + sub], u_band[way, g, line, 8:9])
-                slot = halo * (g % chunks) + k
-                a_send[way, g // chunks, slot:slot + 1] = edge
-            i_send[way, g, halo] = u_band[way, g, 0 if way == 0 else halo, 8:8 + sub]
-
-        for h in range(2):
-            if g == 0:
-                a_send[0, h, 8:8 + band, 0:sub] = k_raw[col, 0:band]
-                a_send[1, h, 8:8 + band, 0:sub] = k_raw[col, sub - band:sub]
+                slot = 5 * ch + k
+                a_send[way, h, slot:slot + 1] = edge
+                far = k - 1 + way
+                if 0 <= far < 2:
+                    n_send[way, g, far] = part.astype(BF16)
+                    slot = 5 * ch + halo + far
+                    a_send[way, h, slot:slot + 1] = jnp.where(col == 0, part[sub - 1:sub], part[0:1])
+            i_send[way, g, halo * way] = u_band[way, g, halo * way, 8:8 + sub]
 
     pl.semaphore_wait(barrier, 1 + 2 * has_up.astype(jnp.int32) + 2 * has_dn.astype(jnp.int32))
 
@@ -218,9 +232,13 @@
         def _():
             for h in range(2):
                 aux_send(way, r_to, h).start()
+            for h in range(2):
+                for ch in range(chunks):
+                    init_send(way, r_to, h, ch, near_rows[way], ir_sem).start()
+                    narrow_send(way, r_to, h, ch).start()
             for ch in range(chunks):
                 for h in range(2):
-                    init_send(way, r_to, h, ch).start()
+                    init_send(way, r_to, h, ch, far_rows[way], far_sem).start()
     kap_pair(col).start()
     u_pair(0, my_cols).start()
     f_pair(0, my_cols).start()
@@ -235,9 +253,9 @@
         for i in range(band, band + sub):
             v_sc[ch, i, 0:8] = jnp.zeros((8, LANES), F32)
             v_sc[ch, i, 8 + wide:16 + wide] = jnp.zeros((8, LANES), F32)
-        e_early[ch, sub - 2:early_rows] = jnp.zeros((early_rows - sub + 2, wide, LANES), BF16)
         return carry
     lax.fori_loop(0, chunks, clear, 0)
+    e_early[sub - 2:early_rows] = jnp.zeros((early_rows - sub + 2, wide, half), BF16)
 
     ext_cells = m_raw.shape[1]
     tile = 256
@@ -319,10 +337,8 @@
                 - fe[rows] * v_sc[ch, mid, left + 1:left + wide + 1])
 
     def first_residual(ch):
-        u_load(ch).wait()
-        f_load(ch).wait()
-        u_pair(ch, other_cols).wait_recv()
-        f_pair(ch, other_cols).wait_recv()
+        local_bytes(u_fin, load_sem.at[ch]).wait()
+        remote_bytes(u_fin, pair_send, pair_recv.at[ch]).wait_recv()
 
         def fill(i, c):
             rows = pl.ds(i * 6, 6)
@@ -338,7 +354,7 @@
         group = (sub - 2) // 2
 
         def to_e(i, c):
-            e_early[ch, pl.ds(i * group, group)] = r_sc[ch, pl.ds(i * group + band, group)].astype(BF16)
+            e_early[pl.ds(i * group, group), :, in_lanes(ch)] = r_sc[ch, pl.ds(i * group + band, group)].astype(BF16)
             return c
         lax.fori_loop(0, 2, to_e, 0)
 
@@ -347,18 +363,22 @@
     mat_pair(other).wait_recv()
     permute(other)
 
-    def early_dot(ch):
+    for ch in range(1, chunks):
+        first_residual(ch)
+
+    def early_dot():
         for side in range(2):
-            operand = e_early[ch, :, 16 * side:16 * side + 32, :].reshape(early_rows * 32, LANES)
-            acc[ch, side] = jnp.dot(m_perm[side, :, late_k:late_k + early_rows * 32], operand,
-                                    preferred_element_type=F32)
+            operand = e_early[:, 16 * side:16 * side + 32, :].reshape(early_rows * 32, half)
+            acc[side] = jnp.dot(m_perm[side, :, late_k:late_k + early_rows * 32], operand,
+                                preferred_element_type=F32)
+
+    early_dot()
 
     for way, present, r_to in ways:
         @pl.when(present)
         def _():
-            for side in range(2):
-                aux_wait(1 - way, r_to, side)
-            put_rows(lambda side, k: a_recv[1 - way, side, 8 + k:9 + k, 0:sub], 0 if way == 0 else band + sub, band)
+            remote_bytes(a_recv.at[1 - way], as_sem.at[way], ar_sem.at[1 - way]).wait_recv()
+            put_rows(lambda side, k: a_recv[1 - way, side, 12 + k:13 + k, 0:sub], 0 if way == 0 else band + sub, band)
 
         @pl.when(jnp.logical_not(present))
         def _():
@@ -380,39 +400,76 @@
         diag_row(i)
         diag_row(ext - 1 - i)
 
+    def side_flux(sent, ch, k, e):
+        slot = pl.ds(5 * ch + k, 1)
+        return fe[e, sub - 1:sub] * (a_recv[sent, 1, slot] - a_recv[sent, 0, slot])
+
+    def near_far(way):
+        if way == 0:
+            return (halo - 1, halo - 1), ((0, 0), (1, 1))
+        return (halo + sub, 0), ((halo + sub + 1, 1), (halo + sub + 2, 2))
+
+    wide_col = lax.broadcasted_iota(jnp.int32, (wide, LANES), 0)
+
     def late_first(ch):
         for way, present, r_to in ways:
             sent = 1 - way
-            rows = pl.ds(0 if way == 0 else halo + sub, halo)
+            (e_near, k_near), far = near_far(way)
+            near_at, u_at = (2, 3) if way == 0 else (1, 0)
 
             @pl.when(present)
             def _():
-                for side in range(2):
-                    init_wait(sent, r_to, ch, side)
-                r_sc[ch, rows] = i_recv[sent, ch, 0:halo]
+                remote_bytes(i_recv.at[sent, ch, 0:3], is_sem.at[way], ir_sem.at[sent, ch]).wait_recv()
+                r_sc[ch, e_near] = i_recv[sent, ch, near_at]
+                flux = side_flux(sent, ch, k_near, e_near)
+                r_sc[ch, e_near, sub - 1:sub] = r_sc[ch, e_near, sub - 1:sub] + flux
+                r_sc[ch, e_near, sub:sub + 1] = r_sc[ch, e_near, sub:sub + 1] - flux
+                for n in range(2):
+                    e, k = far[n]
+                    flux = side_flux(sent, ch, k, e)
+                    slot = pl.ds(5 * ch + halo + n, 1)
+                    got = jnp.concatenate([n_recv[sent, ch, side, n].astype(F32) for side in range(2)], axis=0)
+                    got = jnp.where(wide_col == sub - 1, a_recv[sent, 0, slot] + flux, got)
+                    got = jnp.where(wide_col == sub, a_recv[sent, 1, slot] - flux, got)
+                    e_late[e if way == 0 else e - (ext - 2 * band), :, in_lanes(ch)] = got.astype(BF16)
 
             @pl.when(jnp.logical_not(present))
             def _():
-                i_recv[sent, ch, halo] = jnp.zeros((wide, LANES), F32)
+                i_recv[sent, ch, u_at] = jnp.zeros((wide, LANES), F32)
+                rows = pl.ds(0 if way == 0 else halo + sub, halo)
                 r_sc[ch, rows] = jnp.zeros((halo, wide, LANES), F32)
-
-            for k in range(halo):
-                e = (0 if way == 0 else halo + sub) + k
-                slot = pl.ds(halo * ch + k, 1)
-                flux = fe[e, sub - 1:sub] * (a_recv[sent, 1, slot] - a_recv[sent, 0, slot])
-                r_sc[ch, e, sub - 1:sub] = r_sc[ch, e, sub - 1:sub] + flux
-                r_sc[ch, e, sub:sub + 1] = r_sc[ch, e, sub:sub + 1] - flux
-
-        closed = jnp.where(ch > 0, 1.0, 0.0)
-        flux = fv[halo] * (i_recv[1, ch, halo] - u_sc[ch, 0])
-        r_sc[ch, halo - 1] = r_sc[ch, halo - 1] - flux
-        r_sc[ch, halo] = r_sc[ch, halo] + (flux + closed * (fv[halo] * u_sc[ch, 0]))
-        flux = fv[halo + sub] * (i_recv[0, ch, halo] - u_sc[ch, sub - 1])
-        r_sc[ch, halo + sub] = r_sc[ch, halo + sub] - flux
-        last = halo + sub - 1
-        r_sc[ch, last] = r_sc[ch, last] + (flux + closed * (fv[halo + sub] * u_sc[ch, sub - 1]))
-        e_late[ch, 0:band] = r_sc[ch, 0:band].astype(BF16)
-        e_late[ch, band:2 * band] = r_sc[ch, ext - band:ext].astype(BF16)
+                rows = pl.ds(0 if way == 0 else 2 * band - 2, 2)
+                e_late[rows, :, in_lanes(ch)] = jnp.zeros((2, wide, LANES), BF16)
+
+        flux = fv[halo] * (i_recv[1, ch, 3] - u_sc[ch, 0])
+        near = r_sc[ch, halo - 1] - flux
+        own = r_sc[ch, halo] + flux
+        r_sc[ch, halo - 1] = near
+        r_sc[ch, halo] = own
+        e_late[halo - 1, :, in_lanes(ch)] = near.astype(BF16)
+        e_late[halo, :, in_lanes(ch)] = own.astype(BF16)
+        flux = fv[halo + sub] * (i_recv[0, ch, 0] - u_sc[ch, sub - 1])
+        near = r_sc[ch, halo + sub] - flux
+        own = r_sc[ch, halo + sub - 1] + flux
+        r_sc[ch, halo + sub] = near
+        r_sc[ch, halo + sub - 1] = own
+        e_late[band, :, in_lanes(ch)] = own.astype(BF16)
+        e_late[band + 1, :, in_lanes(ch)] = near.astype(BF16)
+
+    def far_residual(ch):
+        for way, present, r_to in ways:
+            sent = 1 - way
+            _, far = near_far(way)
+
+            @pl.when(present)
+            def _():
+                remote_bytes(i_recv.at[sent, ch, 0:2], is_sem.at[way], far_sem.at[sent, ch]).wait_recv()
+                for n in range(2):
+                    e, k = far[n]
+                    flux = side_flux(sent, ch, k, e)
+                    r_sc[ch, e] = i_recv[sent, ch, n + 2 * way]
+                    r_sc[ch, e, sub - 1:sub] = r_sc[ch, e, sub - 1:sub] + flux
+                    r_sc[ch, e, sub:sub + 1] = r_sc[ch, e, sub:sub + 1] - flux
 
     def update(ch, e, n):
         r_new = r_sc[ch, pl.ds(e, n)] - omega * stencil(ch, e, n)
@@ -425,30 +482,31 @@
             def _():
                 z_copy(t, ch, 1 - way, r_to).wait_recv()
                 at = 0 if way == 0 else band + sub
-                v_sc[ch, at:at + band, left:left + wide] = z_recv[t, ch, 1 - way].astype(F32)
-
-        e_late[ch, 0:band] = update(ch, 0, band).astype(BF16)
-        e_late[ch, band:2 * band] = update(ch, ext - band, band).astype(BF16)
-
-    def solve(ch, side, first, count):
+                v_sc[ch, at:at + band, left:left + wide] = z_recv[1 - way, t, ch].astype(F32)
+
+        e_late[0:band, :, in_lanes(ch)] = update(ch, 0, band).astype(BF16)
+        e_late[band:2 * band, :, in_lanes(ch)] = update(ch, ext - band, band).astype(BF16)
+
+    def solve(lanes, side, first, count):
         lo, n = first * sub, count * sub
         cols = pl.ds(pl.multiple_of(16 * side, 16), 32)
-        operand = e_late[ch, :, cols, :].reshape(late_k, LANES)
-        part = acc[ch, side, lo:lo + n] + jnp.dot(m_perm[side, lo:lo + n, 0:late_k], operand,
-                                                  preferred_element_type=F32)
-        return part.reshape(count, sub, LANES)
-
-    def solve_rows(ch, first, count):
-        return jnp.concatenate([solve(ch, side, first, count) for side in range(2)], axis=1).astype(BF16)
+        operand = e_late[:, cols, lanes]
+        width = operand.shape[2]
+        part = acc[side, lo:lo + n, lanes] + jnp.dot(m_perm[side, lo:lo + n, 0:late_k],
+                                                     operand.reshape(late_k, width), preferred_element_type=F32)
+        return part.reshape(count, sub, width)
+
+    def solve_rows(lanes, first, count):
+        return jnp.concatenate([solve(lanes, side, first, count) for side in range(2)], axis=1).astype(BF16)
 
     def keep_z(ch, first, count, z_bf):
         v_sc[ch, band + first:band + first + count, left:left + wide] = z_bf.astype(F32)
 
     def solve_and_send(t, ch):
-        z_top = solve_rows(ch, 0, band)
-        z_bot = solve_rows(ch, sub - band, band)
-        z_send[t, ch, 0] = z_top
-        z_send[t, ch, 1] = z_bot
+        z_top = solve_rows(in_lanes(ch), 0, band)
+        z_bot = solve_rows(in_lanes(ch), sub - band, band)
+        z_send[0, t, ch] = z_top
+        z_send[1, t, ch] = z_bot
         for way, present, r_to in ways:
             @pl.when(present)
             def _():
@@ -456,39 +514,41 @@
 
         keep_z(ch, 0, band, z_top)
         keep_z(ch, sub - band, band, z_bot)
-        keep_z(ch, band, sub - 2 * band, solve_rows(ch, band, sub - 2 * band))
-
+
+    def interior():
+        z_mid = solve_rows(slice(0, half), band, sub - 2 * band)
+        for ch in range(chunks):
+            keep_z(ch, band, sub - 2 * band, z_mid[:, :, in_lanes(ch)])
         group = (sub - 2) // 2
-
-        def inner(i, c):
-            e_early[ch, pl.ds(i * group, group)] = update(ch, band + i * group, group).astype(BF16)
-            return c
-        lax.fori_loop(0, 2, inner, 0)
-
-        def add(i, c):
-            rows = pl.ds(i * 6, 6)
-            u_sc[ch, rows] = u_sc[ch, rows] + omega * v_sc[ch, pl.ds(i * 6 + band, 6), left:left + wide]
-            return c
-        lax.fori_loop(0, sub // 6, add, 0)
-        early_dot(ch)
-
-    def sweep_first(ch, carry):
-        @pl.when(ch > 0)
-        def _():
-            first_residual(ch)
-        early_dot(ch)
+        for ch in range(chunks):
+            def inner(i, c):
+                e_early[pl.ds(i * group, group), :, in_lanes(ch)] = update(ch, band + i * group, group).astype(BF16)
+                return c
+            lax.fori_loop(0, 2, inner, 0)
+
+            def add(i, c):
+                rows = pl.ds(i * 6, 6)
+                u_sc[ch, rows] = u_sc[ch, rows] + omega * v_sc[ch, pl.ds(i * 6 + band, 6), left:left + wide]
+                return c
+            lax.fori_loop(0, sub // 6, add, 0)
+        early_dot()
+
+    for ch in range(chunks):
         late_first(ch)
         solve_and_send(0, ch)
+    interior()
+
+    def sweep_next(t, carry):
+        @pl.when(t == 0)
+        def _():
+            for ch in range(chunks):
+                far_residual(ch)
+        for ch in range(chunks):
+            late_next(t, ch)
+            solve_and_send(t + 1, ch)
+        interior()
         return carry
-    lax.fori_loop(0, chunks, sweep_first, 0)
-
-    def sweep_next(step, carry):
-        t = step // chunks
-        ch = step % chunks
-        late_next(t, ch)
-        solve_and_send(t + 1, ch)
-        return carry
-    lax.fori_loop(0, (SWEEPS - 2) * chunks, sweep_next, 0)
+    lax.fori_loop(0, SWEEPS - 2, sweep_next, 0)
 
     pieces = 2
     piece = sub // pieces
@@ -497,42 +557,32 @@
         rows = pl.ds(n * piece, piece)
         return pltpu.make_async_remote_copy(
             src_ref=u_fin.at[ch, rows], dst_ref=out_ref.at[rows, :, lanes_of(which, ch)],
-            send_sem=out_send.at[ch, n], recv_sem=out_recv.at[ch, n],
+            send_sem=out_send, recv_sem=out_recv,
             device_id=(other, row), device_id_type=MESH)
 
-    def sweep_last(ch, carry):
+    for ch in range(chunks):
         late_next(SWEEPS - 2, ch)
         for n in range(pieces):
             first = n * piece
-            z = solve(ch, other, first, piece).astype(BF16).astype(F32)
+            z = solve(in_lanes(ch), other, first, piece).astype(BF16).astype(F32)
             u_fin[ch, first:first + piece] = u_sc[ch, first:first + piece, other_cols] + omega * z
             out_pair(ch, n, mine).start()
-        for n in range(pieces):
-            first = n * piece
-            z = solve(ch, col, first, piece).astype(BF16).astype(F32)
-            out_ref[first:first + piece, :, lanes_of(mine, ch)] = u_sc[ch, first:first + piece, my_cols] + omega * z
-        return carry
-    lax.fori_loop(0, chunks, sweep_last, 0)
+    z_own = solve(slice(0, half), col, 0, sub).astype(BF16).astype(F32)
+    for ch in range(chunks):
+        out_ref[:, :, lanes_of(mine, ch)] = u_sc[ch, :, my_cols] + omega * z_own[:, :, in_lanes(ch)]
 
     kap_pair(col).wait_send()
     mat_pair(col).wait_send()
-    for ch in range(chunks):
-        u_pair(ch, my_cols).wait_send()
-        f_pair(ch, my_cols).wait_send()
+    remote_bytes(u_sc, pair_send, pair_recv.at[0]).wait_send()
     for way, present, r_to in ways:
         @pl.when(present)
         def _():
-            for h in range(2):
-                aux_send(way, r_to, h).wait_send()
-                for ch in range(chunks):
-                    init_send(way, r_to, h, ch).wait_send()
-            for ch in range(chunks):
-                for t in range(SWEEPS - 1):
-                    z_copy(t, ch, way, r_to).wait_send()
-    for ch in range(chunks):
-        for n in range(pieces):
-            out_pair(ch, n, mine).wait_send()
-            out_pair(ch, n, theirs).wait_recv()
+            remote_bytes(a_send.at[way], as_sem.at[way], ar_sem.at[way]).wait_send()
+            remote_bytes(i_send.at[way], is_sem.at[way], ir_sem.at[way, 0]).wait_send()
+            remote_bytes(n_send.at[way], ns_sem.at[way], ir_sem.at[way, 0]).wait_send()
+            remote_bytes(z_send.at[way], zs_sem.at[way], zr_sem.at[0, 0, way]).wait_send()
+    remote_bytes(u_fin, out_send, out_recv).wait_send()
+    remote_bytes(u_fin, out_send, out_recv).wait_recv()
 
 
 def solution(mesh):
@@ -560,9 +610,9 @@
                 vmem((chunks, sub, wide, LANES), F32),
                 vmem((chunks, ext, wide, LANES), F32),
                 vmem((chunks, ext + 2, 64, LANES), F32),
-                vmem((chunks, 2 * band, wide, LANES), BF16),
-                vmem((chunks, early_rows, wide, LANES), BF16),
-                vmem((chunks, 2, sub * sub, LANES), F32),
+                vmem((2 * band, wide, chunks * LANES), BF16),
+                vmem((early_rows, wide, chunks * LANES), BF16),
+                vmem((2, sub * sub, chunks * LANES), F32),
                 vmem((2, ext_cells, sub * sub), BF16),
                 vmem((sub * sub, 1024), BF16),
                 vmem((2, sub * sub, 1024), BF16),
@@ -580,16 +630,16 @@
                 vmem((2, halo, sub, LANES), F32),
                 vmem((2, 2 * chunks, band, sub, LANES), F32),
                 vmem((2, chunks, band, wide, LANES), F32),
+                vmem((2, 2 * chunks, 2, sub, LANES), BF16),
+                vmem((2, chunks, 2, 2, sub, LANES), BF16),
                 vmem((2, 2, 16, LANES), F32),
                 vmem((2, 2, 16, LANES), F32),
-                vmem((SWEEPS - 1, chunks, 2, band, wide, LANES), BF16),
-                vmem((SWEEPS - 1, chunks, 2, band, wide, LANES), BF16),
+                vmem((2, SWEEPS - 1, chunks, band, wide, LANES), BF16),
+                vmem((2, SWEEPS - 1, chunks, band, wide, LANES), BF16),
                 vmem((chunks, sub, sub, LANES), F32),
-                dma((2, chunks)), dma((2, 2, 2 * chunks)), dma((3, chunks)), dma((3, chunks)), dma, dma,
-                dma, dma,
-                dma((2, 2 * chunks)), dma((2, chunks, 2)), dma((2, 2)), dma((2, 2)),
-                dma((SWEEPS - 1, chunks, 2)), dma((SWEEPS - 1, chunks, 2)),
-                dma((chunks, 2)), dma((chunks, 2)),
+                dma((chunks,)), dma((2,)), dma, dma((chunks,)), dma, dma, dma, dma, dma, dma,
+                dma((2,)), dma((2,)), dma((2, chunks)), dma((2, chunks)), dma((2,)), dma((2,)),
+                dma((2,)), dma((2, chunks, 2)), dma, dma,
             ],
             compiler_params=pltpu.CompilerParams(collective_id=0, has_side_effects=True,
                                                  vmem_limit_bytes=61000 * 1024),

time: 45.1 us -> 43.5 us (0.965)
  Pallas kernels: 43.2 us -> 41.6 us
    pallas_call x1, Pallas kernels: 43.2 us -> 41.6 us  [device_fn(): pl.pallas_call(functools.partial(kernel, row_count, sub, halo, chunks), o...]
where the time goes in v3:
time: 43.5 us; the launch traced here: 43.3 us
  Pallas kernels  41.6 us (96%)
  local copies, waits for them, and re-layouts  1.02 us (2%)
  between operations  0.66 us (2%)
    pallas_call x1, Pallas kernels, device_fn(): pl.pallas_call(functools.partial(kernel, row_count, sub, halo, chunks), o...  41.6 us
    unnamed x1, local copies, waits for them, and re-layouts  1.02 us

profile of v3, /device:TPU:97, one launch (start us, length us, event | category | flops | bytes accessed | tf_op | source)
XLA Modules:
  0.0 43.3 jit_solution(10391023314068999395)
XLA Ops:
  0.7 41.6 %shard_map.55 = f32[24,24,512]{2,1,0:T(8,128)S(1)} custom-call(f32[1]{0:T(128)} %bitcast.4.om_ref, f32[24,24,512]{2,1,0:T(8,128)} %f_hbm.1, f32[24,24,512]{2,1,0:T(8,128)} %u_hbm.1, f32[24,24]{1,0:T(8,128)} %kap_hbm.1, bf16[900,576]{1,0:T(8,128)(2,1)} %bitcast.5), custom_call_target="tpu_custom_call" | custom-call | tf_op jit(solution)/shard_map/pallas_call | solution.py:604
  42.3 1.0 %copy.7 = f32[24,24,512]{2,1,0:T(8,128)} copy(f32[24,24,512]{2,1,0:T(8,128)S(1)} %shard_map.55) | data formatting | bytes 2359296

commit v4 on v3

--- a/solution.py
+++ b/solution.py
@@ -9,6 +9,7 @@
 from jax.sharding import PartitionSpec as P
 
 SWEEPS = 6
+ORDER = (((1, 0, 0), (1, 0, 1), (0, 0, 0), (1, 1, 0), (1, 1, 1), (0, 0, 1), (0, 1, 0), (0, 1, 1)), ((1, 1, 0), (1, 1, 1), (1, 0, 0), (1, 0, 1), (0, 1, 0), (0, 1, 1), (0, 0, 0), (0, 0, 1)))
 LANES = 128
 MESH = pl.DeviceIdType.MESH
 F32 = jnp.float32
@@ -21,7 +22,7 @@
            k_raw, kb, ko, fv, fw, fe, dg, u_band, pv, pw, pe, pd, i_send, i_recv, n_send, n_recv, a_send, a_recv,
            z_send, z_recv, u_fin,
            load_sem, band_sem, pair_send, pair_recv, mat_sem, mat_send, mat_recv, kap_loc, kap_send, kap_recv,
-           is_sem, ns_sem, ir_sem, far_sem, as_sem, ar_sem, zs_sem, zr_sem, out_send, out_recv):
+           ici_sem, ir_sem, far_sem, ar_sem, zr_sem, out_recv):
     wide = 2 * sub
     ext = sub + 2 * halo
     band = halo + 1
@@ -77,9 +78,9 @@
         u_from = pl.ds(0 if way == 0 else sub - band, band)
         f_from = pl.ds(0 if way == 0 else sub - halo, halo)
         return (pltpu.make_async_copy(u_hbm.at[u_from, :, lanes], u_band.at[way, g, :, 8:8 + sub, :],
-                                      band_sem.at[0]),
+                                      band_sem),
                 pltpu.make_async_copy(f_hbm.at[f_from, :, lanes], i_send.at[way, g, pl.ds(1 - way, halo)],
-                                      band_sem.at[1]))
+                                      band_sem))
 
     for g in range(2 * chunks):
         for way in range(2):
@@ -87,11 +88,11 @@
                 load.start()
 
     def u_load(ch):
-        return pltpu.make_async_copy(u_hbm.at[:, :, lanes_of(mine, ch)], u_sc.at[ch, :, my_cols, :], load_sem.at[ch])
+        return pltpu.make_async_copy(u_hbm.at[:, :, lanes_of(mine, ch)], u_sc.at[ch, :, my_cols, :], load_sem)
 
     def f_load(ch):
         return pltpu.make_async_copy(f_hbm.at[:, :, lanes_of(mine, ch)], r_sc.at[ch, own_rows, my_cols, :],
-                                     load_sem.at[ch])
+                                     load_sem)
 
     mat_load = pltpu.make_async_copy(mat_hbm, m_raw.at[col], mat_sem)
     mat_load.start()
@@ -123,35 +124,35 @@
             send_sem=kap_send, recv_sem=kap_recv,
             device_id=(other, row), device_id_type=MESH)
 
-    def core_for(h):
-        return lax.rem(h + row + 1, 2)
+    def half_at(core):
+        return lax.rem(core + row + 1, 2)
 
     near_rows = (pl.ds(0, 2), pl.ds(2, 2))
     far_rows = (pl.ds(2, 2), pl.ds(0, 2))
 
-    def init_send(way, r_to, h, ch, rows, recv_sem):
-        g = h * chunks + ch
+    def init_send(way, r_to, core, ch, rows, recv_sem):
+        g = half_at(core) * chunks + ch
         return pltpu.make_async_remote_copy(
             src_ref=i_send.at[way, g, rows], dst_ref=i_recv.at[way, ch, rows, my_cols, :],
-            send_sem=is_sem.at[way], recv_sem=recv_sem.at[way, ch],
-            device_id=(core_for(h), r_to), device_id_type=MESH)
-
-    def narrow_send(way, r_to, h, ch):
-        return pltpu.make_async_remote_copy(
-            src_ref=n_send.at[way, h * chunks + ch], dst_ref=n_recv.at[way, ch, col],
-            send_sem=ns_sem.at[way], recv_sem=ir_sem.at[way, ch],
-            device_id=(core_for(h), r_to), device_id_type=MESH)
-
-    def aux_send(way, r_to, h):
-        return pltpu.make_async_remote_copy(
-            src_ref=a_send.at[way, h], dst_ref=a_recv.at[way, col],
-            send_sem=as_sem.at[way], recv_sem=ar_sem.at[way],
-            device_id=(core_for(h), r_to), device_id_type=MESH)
+            send_sem=ici_sem.at[way], recv_sem=recv_sem,
+            device_id=(core, r_to), device_id_type=MESH)
+
+    def narrow_send(way, r_to, core, ch):
+        return pltpu.make_async_remote_copy(
+            src_ref=n_send.at[way, half_at(core) * chunks + ch], dst_ref=n_recv.at[way, ch, col],
+            send_sem=ici_sem.at[way], recv_sem=ir_sem.at[way, ch],
+            device_id=(core, r_to), device_id_type=MESH)
+
+    def aux_send(way, r_to, core):
+        return pltpu.make_async_remote_copy(
+            src_ref=a_send.at[way, half_at(core)], dst_ref=a_recv.at[way, col],
+            send_sem=ici_sem.at[way], recv_sem=ar_sem.at[way],
+            device_id=(core, r_to), device_id_type=MESH)
 
     def z_copy(t, ch, way, r_to):
         return pltpu.make_async_remote_copy(
             src_ref=z_send.at[way, t, ch], dst_ref=z_recv.at[way, t, ch],
-            send_sem=zs_sem.at[way], recv_sem=zr_sem.at[t % 2, ch, way],
+            send_sem=ici_sem.at[way], recv_sem=zr_sem.at[t % 2, ch, way],
             device_id=(other, r_to), device_id_type=MESH)
 
     omega = om_ref[0]
@@ -193,8 +194,7 @@
                 total = total + pv[way, k + 1]
             pd[way, k] = total
 
-    local_bytes(i_send, band_sem.at[0]).wait()
-    local_bytes(i_send.at[:, :, 0:halo], band_sem.at[1]).wait()
+    local_bytes(v_sc.at[0, 0:21], band_sem).wait()
     for way in range(2):
         for h in range(2):
             first = 0 if way == 0 else sub - band
@@ -230,15 +230,14 @@
     for way, present, r_to in ways:
         @pl.when(present)
         def _():
-            for h in range(2):
-                aux_send(way, r_to, h).start()
-            for h in range(2):
-                for ch in range(chunks):
-                    init_send(way, r_to, h, ch, near_rows[way], ir_sem).start()
-                    narrow_send(way, r_to, h, ch).start()
-            for ch in range(chunks):
-                for h in range(2):
-                    init_send(way, r_to, h, ch, far_rows[way], far_sem).start()
+            for core in range(2):
+                aux_send(way, r_to, core).start()
+            for near, core, ch in ORDER[way]:
+                if near:
+                    init_send(way, r_to, core, ch, near_rows[way], ir_sem.at[way, ch]).start()
+                    narrow_send(way, r_to, core, ch).start()
+                else:
+                    init_send(way, r_to, core, ch, far_rows[way], far_sem.at[way]).start()
     kap_pair(col).start()
     u_pair(0, my_cols).start()
     f_pair(0, my_cols).start()
@@ -336,8 +335,9 @@
                 - fw[rows] * v_sc[ch, mid, left - 1:left + wide - 1]
                 - fe[rows] * v_sc[ch, mid, left + 1:left + wide + 1])
 
+    local_bytes(u_sc, load_sem).wait()
+
     def first_residual(ch):
-        local_bytes(u_fin, load_sem.at[ch]).wait()
         remote_bytes(u_fin, pair_send, pair_recv.at[ch]).wait_recv()
 
         def fill(i, c):
@@ -377,7 +377,7 @@
     for way, present, r_to in ways:
         @pl.when(present)
         def _():
-            remote_bytes(a_recv.at[1 - way], as_sem.at[way], ar_sem.at[1 - way]).wait_recv()
+            remote_bytes(a_recv.at[1 - way], ici_sem.at[way], ar_sem.at[1 - way]).wait_recv()
             put_rows(lambda side, k: a_recv[1 - way, side, 12 + k:13 + k, 0:sub], 0 if way == 0 else band + sub, band)
 
         @pl.when(jnp.logical_not(present))
@@ -419,7 +419,7 @@
 
             @pl.when(present)
             def _():
-                remote_bytes(i_recv.at[sent, ch, 0:3], is_sem.at[way], ir_sem.at[sent, ch]).wait_recv()
+                remote_bytes(i_recv.at[sent, ch, 0:3], ici_sem.at[way], ir_sem.at[sent, ch]).wait_recv()
                 r_sc[ch, e_near] = i_recv[sent, ch, near_at]
                 flux = side_flux(sent, ch, k_near, e_near)
                 r_sc[ch, e_near, sub - 1:sub] = r_sc[ch, e_near, sub - 1:sub] + flux
@@ -456,20 +456,26 @@
         e_late[band, :, in_lanes(ch)] = own.astype(BF16)
         e_late[band + 1, :, in_lanes(ch)] = near.astype(BF16)
 
-    def far_residual(ch):
+    def far_wait():
+        for way, present, r_to in ways:
+            @pl.when(present)
+            def _():
+                remote_bytes(i_recv.at[1 - way, :, 0:2], ici_sem.at[way], far_sem.at[1 - way]).wait_recv()
+
+    def far_residual():
         for way, present, r_to in ways:
             sent = 1 - way
             _, far = near_far(way)
 
             @pl.when(present)
             def _():
-                remote_bytes(i_recv.at[sent, ch, 0:2], is_sem.at[way], far_sem.at[sent, ch]).wait_recv()
-                for n in range(2):
-                    e, k = far[n]
-                    flux = side_flux(sent, ch, k, e)
-                    r_sc[ch, e] = i_recv[sent, ch, n + 2 * way]
-                    r_sc[ch, e, sub - 1:sub] = r_sc[ch, e, sub - 1:sub] + flux
-                    r_sc[ch, e, sub:sub + 1] = r_sc[ch, e, sub:sub + 1] - flux
+                for ch in range(chunks):
+                    for n in range(2):
+                        e, k = far[n]
+                        flux = side_flux(sent, ch, k, e)
+                        r_sc[ch, e] = i_recv[sent, ch, n + 2 * way]
+                        r_sc[ch, e, sub - 1:sub] = r_sc[ch, e, sub - 1:sub] + flux
+                        r_sc[ch, e, sub:sub + 1] = r_sc[ch, e, sub:sub + 1] - flux
 
     def update(ch, e, n):
         r_new = r_sc[ch, pl.ds(e, n)] - omega * stencil(ch, e, n)
@@ -541,8 +547,8 @@
     def sweep_next(t, carry):
         @pl.when(t == 0)
         def _():
-            for ch in range(chunks):
-                far_residual(ch)
+            far_wait()
+            far_residual()
         for ch in range(chunks):
             late_next(t, ch)
             solve_and_send(t + 1, ch)
@@ -557,7 +563,7 @@
         rows = pl.ds(n * piece, piece)
         return pltpu.make_async_remote_copy(
             src_ref=u_fin.at[ch, rows], dst_ref=out_ref.at[rows, :, lanes_of(which, ch)],
-            send_sem=out_send, recv_sem=out_recv,
+            send_sem=pair_send, recv_sem=out_recv,
             device_id=(other, row), device_id_type=MESH)
 
     for ch in range(chunks):
@@ -573,16 +579,12 @@
 
     kap_pair(col).wait_send()
     mat_pair(col).wait_send()
-    remote_bytes(u_sc, pair_send, pair_recv.at[0]).wait_send()
     for way, present, r_to in ways:
         @pl.when(present)
         def _():
-            remote_bytes(a_send.at[way], as_sem.at[way], ar_sem.at[way]).wait_send()
-            remote_bytes(i_send.at[way], is_sem.at[way], ir_sem.at[way, 0]).wait_send()
-            remote_bytes(n_send.at[way], ns_sem.at[way], ir_sem.at[way, 0]).wait_send()
-            remote_bytes(z_send.at[way], zs_sem.at[way], zr_sem.at[0, 0, way]).wait_send()
-    remote_bytes(u_fin, out_send, out_recv).wait_send()
-    remote_bytes(u_fin, out_send, out_recv).wait_recv()
+            remote_bytes(v_sc.at[0, 0:23], ici_sem.at[way], ar_sem.at[way]).wait_send()
+    remote_bytes(u_fin, pair_send, out_recv).wait_recv()
+    remote_bytes(v_sc.at[:, 0:27], pair_send, out_recv).wait_send()
 
 
 def solution(mesh):
@@ -637,9 +639,8 @@
                 vmem((2, SWEEPS - 1, chunks, band, wide, LANES), BF16),
                 vmem((2, SWEEPS - 1, chunks, band, wide, LANES), BF16),
                 vmem((chunks, sub, sub, LANES), F32),
-                dma((chunks,)), dma((2,)), dma, dma((chunks,)), dma, dma, dma, dma, dma, dma,
-                dma((2,)), dma((2,)), dma((2, chunks)), dma((2, chunks)), dma((2,)), dma((2,)),
-                dma((2,)), dma((2, chunks, 2)), dma, dma,
+                dma, dma, dma, dma((chunks,)), dma, dma, dma, dma, dma, dma,
+                dma((2,)), dma((2, chunks)), dma((2,)), dma((2,)), dma((2, chunks, 2)), dma,
             ],
             compiler_params=pltpu.CompilerParams(collective_id=0, has_side_effects=True,
                                                  vmem_limit_bytes=61000 * 1024),

time: 43.5 us -> 43 us (0.989)
  Pallas kernels: 41.6 us -> 41.1 us
    pallas_call x1, Pallas kernels: 41.6 us -> 41.1 us  [device_fn(): pl.pallas_call(functools.partial(kernel, row_count, sub, halo, chunks), o...]
where the time goes in v4:
time: 43 us; the launch traced here: 42.8 us
  Pallas kernels  41.1 us (96%)
  local copies, waits for them, and re-layouts  1.02 us (2%)
  between operations  0.66 us (2%)
    pallas_call x1, Pallas kernels, device_fn(): pl.pallas_call(functools.partial(kernel, row_count, sub, halo, chunks), o...  41.1 us
    unnamed x1, local copies, waits for them, and re-layouts  1.02 us

profile of v4, /device:TPU:97, one launch (start us, length us, event | category | flops | bytes accessed | tf_op | source)
XLA Modules:
  0.0 42.8 jit_solution(6891258025830048878)
XLA Ops:
  0.7 41.1 %shard_map.55 = f32[24,24,512]{2,1,0:T(8,128)S(1)} custom-call(f32[1]{0:T(128)} %bitcast.4.om_ref, f32[24,24,512]{2,1,0:T(8,128)} %f_hbm.1, f32[24,24,512]{2,1,0:T(8,128)} %u_hbm.1, f32[24,24]{1,0:T(8,128)} %kap_hbm.1, bf16[900,576]{1,0:T(8,128)(2,1)} %bitcast.5), custom_call_target="tpu_custom_call" | custom-call | tf_op jit(solution)/shard_map/pallas_call | solution.py:606
  41.8 1.0 %copy.7 = f32[24,24,512]{2,1,0:T(8,128)} copy(f32[24,24,512]{2,1,0:T(8,128)S(1)} %shard_map.55) | data formatting | bytes 2359296

commit v5 on v4

--- a/solution.py
+++ b/solution.py
@@ -482,23 +482,29 @@
         r_sc[ch, pl.ds(e, n)] = r_new
         return r_new
 
+    slow = lax.rem(row, 2)
+
+    def towards(way):
+        return jnp.where(way == 0, has_up, has_dn), jnp.where(way == 0, up_row, dn_row)
+
     def late_next(t, ch):
-        for way, present, r_to in ways:
+        for way in (1 - slow, slow):
+            present, r_to = towards(way)
+
             @pl.when(present)
             def _():
                 z_copy(t, ch, 1 - way, r_to).wait_recv()
-                at = 0 if way == 0 else band + sub
-                v_sc[ch, at:at + band, left:left + wide] = z_recv[1 - way, t, ch].astype(F32)
-
-        e_late[0:band, :, in_lanes(ch)] = update(ch, 0, band).astype(BF16)
-        e_late[band:2 * band, :, in_lanes(ch)] = update(ch, ext - band, band).astype(BF16)
+                v_sc[ch, pl.ds(way * (band + sub), band), left:left + wide] = z_recv[1 - way, t, ch].astype(F32)
+
+            e_late[pl.ds(way * band, band), :, in_lanes(ch)] = update(ch, way * (ext - band), band).astype(BF16)
 
     def solve(lanes, side, first, count):
-        lo, n = first * sub, count * sub
+        n = count * sub
+        rows = pl.ds(first * sub if isinstance(first, int) else pl.multiple_of(first * sub, 32), n)
         cols = pl.ds(pl.multiple_of(16 * side, 16), 32)
         operand = e_late[:, cols, lanes]
         width = operand.shape[2]
-        part = acc[side, lo:lo + n, lanes] + jnp.dot(m_perm[side, lo:lo + n, 0:late_k],
+        part = acc[side, rows, lanes] + jnp.dot(m_perm[side, rows, 0:late_k],
                                                      operand.reshape(late_k, width), preferred_element_type=F32)
         return part.reshape(count, sub, width)
 
@@ -506,20 +512,20 @@
         return jnp.concatenate([solve(lanes, side, first, count) for side in range(2)], axis=1).astype(BF16)
 
     def keep_z(ch, first, count, z_bf):
-        v_sc[ch, band + first:band + first + count, left:left + wide] = z_bf.astype(F32)
+        v_sc[ch, pl.ds(band + first, count), left:left + wide] = z_bf.astype(F32)
 
     def solve_and_send(t, ch):
-        z_top = solve_rows(in_lanes(ch), 0, band)
-        z_bot = solve_rows(in_lanes(ch), sub - band, band)
-        z_send[0, t, ch] = z_top
-        z_send[1, t, ch] = z_bot
-        for way, present, r_to in ways:
+        for way in (slow, 1 - slow):
+            present, r_to = towards(way)
+            first = way * (sub - band)
+            z_bf = solve_rows(in_lanes(ch), first, band)
+            z_send[way, t, ch] = z_bf
+
             @pl.when(present)
             def _():
                 z_copy(t, ch, way, r_to).start()
 
-        keep_z(ch, 0, band, z_top)
-        keep_z(ch, sub - band, band, z_bot)
+            keep_z(ch, first, band, z_bf)
 
     def interior():
         z_mid = solve_rows(slice(0, half), band, sub - 2 * band)
@@ -556,11 +562,10 @@
         return carry
     lax.fori_loop(0, SWEEPS - 2, sweep_next, 0)
 
-    pieces = 2
-    piece = sub // pieces
+    cuts = (0, 16, sub)
 
     def out_pair(ch, n, which):
-        rows = pl.ds(n * piece, piece)
+        rows = pl.ds(cuts[n], cuts[n + 1] - cuts[n])
         return pltpu.make_async_remote_copy(
             src_ref=u_fin.at[ch, rows], dst_ref=out_ref.at[rows, :, lanes_of(which, ch)],
             send_sem=pair_send, recv_sem=out_recv,
@@ -568,10 +573,10 @@
 
     for ch in range(chunks):
         late_next(SWEEPS - 2, ch)
-        for n in range(pieces):
-            first = n * piece
-            z = solve(in_lanes(ch), other, first, piece).astype(BF16).astype(F32)
-            u_fin[ch, first:first + piece] = u_sc[ch, first:first + piece, other_cols] + omega * z
+        for n in range(2):
+            first, past = cuts[n], cuts[n + 1]
+            z = solve(in_lanes(ch), other, first, past - first).astype(BF16).astype(F32)
+            u_fin[ch, first:past] = u_sc[ch, first:past, other_cols] + omega * z
             out_pair(ch, n, mine).start()
     z_own = solve(slice(0, half), col, 0, sub).astype(BF16).astype(F32)
     for ch in range(chunks):

time: 43 us -> 42.6 us (level)
  no operation moved by 1% of the time
where the time goes in v5:
time: 42.6 us; the launch traced here: 42.4 us
  Pallas kernels  40.7 us (96%)
  local copies, waits for them, and re-layouts  1.02 us (2%)
  between operations  0.66 us (2%)
    pallas_call x1, Pallas kernels, device_fn(): pl.pallas_call(functools.partial(kernel, row_count, sub, halo, chunks), o...  40.7 us
    unnamed x1, local copies, waits for them, and re-layouts  1.02 us

profile of v5, /device:TPU:97, one launch (start us, length us, event | category | flops | bytes accessed | tf_op | source)
XLA Modules:
  0.0 42.4 jit_solution(4047281174763176459)
XLA Ops:
  0.7 40.7 %shard_map.55 = f32[24,24,512]{2,1,0:T(8,128)S(1)} custom-call(f32[1]{0:T(128)} %bitcast.4.om_ref, f32[24,24,512]{2,1,0:T(8,128)} %f_hbm.1, f32[24,24,512]{2,1,0:T(8,128)} %u_hbm.1, f32[24,24]{1,0:T(8,128)} %kap_hbm.1, bf16[900,576]{1,0:T(8,128)(2,1)} %bitcast.5), custom_call_target="tpu_custom_call" | custom-call | tf_op jit(solution)/shard_map/pallas_call | solution.py:611
  41.4 1.0 %copy.7 = f32[24,24,512]{2,1,0:T(8,128)} copy(f32[24,24,512]{2,1,0:T(8,128)S(1)} %shard_map.55) | data formatting | bytes 2359296

commit v6 on v5

--- a/solution.py
+++ b/solution.py
@@ -9,7 +9,6 @@
 from jax.sharding import PartitionSpec as P
 
 SWEEPS = 6
-ORDER = (((1, 0, 0), (1, 0, 1), (0, 0, 0), (1, 1, 0), (1, 1, 1), (0, 0, 1), (0, 1, 0), (0, 1, 1)), ((1, 1, 0), (1, 1, 1), (1, 0, 0), (1, 0, 1), (0, 1, 0), (0, 1, 1), (0, 0, 0), (0, 0, 1)))
 LANES = 128
 MESH = pl.DeviceIdType.MESH
 F32 = jnp.float32
@@ -230,14 +229,29 @@
     for way, present, r_to in ways:
         @pl.when(present)
         def _():
-            for core in range(2):
-                aux_send(way, r_to, core).start()
-            for near, core, ch in ORDER[way]:
-                if near:
-                    init_send(way, r_to, core, ch, near_rows[way], ir_sem.at[way, ch]).start()
-                    narrow_send(way, r_to, core, ch).start()
-                else:
-                    init_send(way, r_to, core, ch, far_rows[way], far_sem.at[way]).start()
+            def near(core, ch):
+                init_send(way, r_to, core, ch, near_rows[way], ir_sem.at[way, ch]).start()
+                narrow_send(way, r_to, core, ch).start()
+
+            def far(core, ch, n):
+                rows = pl.ds((2, 0)[way] + n, 1)
+                init_send(way, r_to, core, ch, rows, far_sem.at[way]).start()
+
+            first, second = way, 1 - way
+            aux_send(way, r_to, first).start()
+            for ch in range(chunks):
+                near(first, ch)
+            far(first, 0, 0)
+            aux_send(way, r_to, second).start()
+            for ch in range(chunks):
+                near(second, ch)
+            far(first, 0, 1)
+            for ch in range(1, chunks):
+                far(first, ch, 0)
+                far(first, ch, 1)
+            for ch in range(chunks):
+                far(second, ch, 0)
+                far(second, ch, 1)
     kap_pair(col).start()
     u_pair(0, my_cols).start()
     f_pair(0, my_cols).start()

time: 42.6 us -> 42.3 us (level)
  no operation moved by 1% of the time
where the time goes in v6:
time: 42.3 us; the launch traced here: 42.2 us
  Pallas kernels  40.5 us (96%)
  local copies, waits for them, and re-layouts  1.02 us (2%)
  between operations  0.66 us (2%)
    pallas_call x1, Pallas kernels, device_fn(): pl.pallas_call(functools.partial(kernel, row_count, sub, halo, chunks), o...  40.5 us
    unnamed x1, local copies, waits for them, and re-layouts  1.02 us

profile of v6, /device:TPU:97, one launch (start us, length us, event | category | flops | bytes accessed | tf_op | source)
XLA Modules:
  0.0 42.2 jit_solution(82689771239500466)
XLA Ops:
  0.7 40.5 %shard_map.55 = f32[24,24,512]{2,1,0:T(8,128)S(1)} custom-call(f32[1]{0:T(128)} %bitcast.4.om_ref, f32[24,24,512]{2,1,0:T(8,128)} %f_hbm.1, f32[24,24,512]{2,1,0:T(8,128)} %u_hbm.1, f32[24,24]{1,0:T(8,128)} %kap_hbm.1, bf16[900,576]{1,0:T(8,128)(2,1)} %bitcast.5), custom_call_target="tpu_custom_call" | custom-call | tf_op jit(solution)/shard_map/pallas_call | solution.py:625
  41.1 1.0 %copy.7 = f32[24,24,512]{2,1,0:T(8,128)} copy(f32[24,24,512]{2,1,0:T(8,128)S(1)} %shard_map.55) | data formatting | bytes 2359296

commit v7 on v6

--- a/solution.py
+++ b/solution.py
@@ -455,20 +455,14 @@
                 rows = pl.ds(0 if way == 0 else 2 * band - 2, 2)
                 e_late[rows, :, in_lanes(ch)] = jnp.zeros((2, wide, LANES), BF16)
 
-        flux = fv[halo] * (i_recv[1, ch, 3] - u_sc[ch, 0])
-        near = r_sc[ch, halo - 1] - flux
-        own = r_sc[ch, halo] + flux
-        r_sc[ch, halo - 1] = near
-        r_sc[ch, halo] = own
-        e_late[halo - 1, :, in_lanes(ch)] = near.astype(BF16)
-        e_late[halo, :, in_lanes(ch)] = own.astype(BF16)
-        flux = fv[halo + sub] * (i_recv[0, ch, 0] - u_sc[ch, sub - 1])
-        near = r_sc[ch, halo + sub] - flux
-        own = r_sc[ch, halo + sub - 1] + flux
-        r_sc[ch, halo + sub] = near
-        r_sc[ch, halo + sub - 1] = own
-        e_late[band, :, in_lanes(ch)] = own.astype(BF16)
-        e_late[band + 1, :, in_lanes(ch)] = near.astype(BF16)
+            face, e_own, own_line = (halo, halo, 0) if way == 0 else (halo + sub, halo + sub - 1, sub - 1)
+            flux = fv[face] * (i_recv[sent, ch, u_at] - u_sc[ch, own_line])
+            near = r_sc[ch, e_near] - flux
+            own = r_sc[ch, e_own] + flux
+            r_sc[ch, e_near] = near
+            r_sc[ch, e_own] = own
+            e_late[halo - 1 if way == 0 else band + 1, :, in_lanes(ch)] = near.astype(BF16)
+            e_late[halo if way == 0 else band, :, in_lanes(ch)] = own.astype(BF16)
 
     def far_wait():
         for way, present, r_to in ways:
@@ -501,8 +495,8 @@
     def towards(way):
         return jnp.where(way == 0, has_up, has_dn), jnp.where(way == 0, up_row, dn_row)
 
-    def late_next(t, ch):
-        for way in (1 - slow, slow):
+    def late_next(t, ch, ahead):
+        for n, way in enumerate((1 - slow, slow)):
             present, r_to = towards(way)
 
             @pl.when(present)
@@ -511,28 +505,36 @@
                 v_sc[ch, pl.ds(way * (band + sub), band), left:left + wide] = z_recv[1 - way, t, ch].astype(F32)
 
             e_late[pl.ds(way * band, band), :, in_lanes(ch)] = update(ch, way * (ext - band), band).astype(BF16)
-
-    def solve(lanes, side, first, count):
+            if n == 0 and ahead:
+                first = slow * (sub - band)
+                rows = pl.ds(pl.multiple_of(first * sub, 32), band * sub)
+                for side in range(2):
+                    acc[side, rows, in_lanes(ch)] = solve(in_lanes(ch), side, first, band, way).reshape(band * sub, LANES)
+
+    def solve(lanes, side, first, count, only=None):
         n = count * sub
         rows = pl.ds(first * sub if isinstance(first, int) else pl.multiple_of(first * sub, 32), n)
         cols = pl.ds(pl.multiple_of(16 * side, 16), 32)
-        operand = e_late[:, cols, lanes]
+        lines = slice(None) if only is None else pl.ds(only * band, band)
+        depth = late_k if only is None else late_k // 2
+        at = 0 if only is None else pl.multiple_of(only * depth, depth)
+        operand = e_late[lines, cols, lanes]
         width = operand.shape[2]
-        part = acc[side, rows, lanes] + jnp.dot(m_perm[side, rows, 0:late_k],
-                                                     operand.reshape(late_k, width), preferred_element_type=F32)
+        part = acc[side, rows, lanes] + jnp.dot(m_perm[side, rows, pl.ds(at, depth)],
+                                                     operand.reshape(depth, width), preferred_element_type=F32)
         return part.reshape(count, sub, width)
 
-    def solve_rows(lanes, first, count):
-        return jnp.concatenate([solve(lanes, side, first, count) for side in range(2)], axis=1).astype(BF16)
+    def solve_rows(lanes, first, count, only=None):
+        return jnp.concatenate([solve(lanes, side, first, count, only) for side in range(2)], axis=1).astype(BF16)
 
     def keep_z(ch, first, count, z_bf):
         v_sc[ch, pl.ds(band + first, count), left:left + wide] = z_bf.astype(F32)
 
-    def solve_and_send(t, ch):
-        for way in (slow, 1 - slow):
+    def solve_and_send(t, ch, left_way):
+        for n, way in enumerate((slow, 1 - slow)):
             present, r_to = towards(way)
             first = way * (sub - band)
-            z_bf = solve_rows(in_lanes(ch), first, band)
+            z_bf = solve_rows(in_lanes(ch), first, band, left_way if n == 0 else None)
             z_send[way, t, ch] = z_bf
 
             @pl.when(present)
@@ -561,7 +563,7 @@
 
     for ch in range(chunks):
         late_first(ch)
-        solve_and_send(0, ch)
+        solve_and_send(0, ch, None)
     interior()
 
     def sweep_next(t, carry):
@@ -570,8 +572,8 @@
             far_wait()
             far_residual()
         for ch in range(chunks):
-            late_next(t, ch)
-            solve_and_send(t + 1, ch)
+            late_next(t, ch, True)
+            solve_and_send(t + 1, ch, slow)
         interior()
         return carry
     lax.fori_loop(0, SWEEPS - 2, sweep_next, 0)
@@ -586,7 +588,7 @@
             device_id=(other, row), device_id_type=MESH)
 
     for ch in range(chunks):
-        late_next(SWEEPS - 2, ch)
+        late_next(SWEEPS - 2, ch, False)
         for n in range(2):
             first, past = cuts[n], cuts[n + 1]
             z = solve(in_lanes(ch), other, first, past - first).astype(BF16).astype(F32)

time: 42.3 us -> 42.2 us (level)
  no operation moved by 1% of the time
where the time goes in v7:
time: 42.2 us; the launch traced here: 42.1 us
  Pallas kernels  40.4 us (96%)
  local copies, waits for them, and re-layouts  1.02 us (2%)
  between operations  0.66 us (2%)
    pallas_call x1, Pallas kernels, device_fn(): pl.pallas_call(functools.partial(kernel, row_count, sub, halo, chunks), o...  40.4 us
    unnamed x1, local copies, waits for them, and re-layouts  1.02 us

profile of v7, /device:TPU:97, one launch (start us, length us, event | category | flops | bytes accessed | tf_op | source)
XLA Modules:
  0.0 42.1 jit_solution(4953349606595343960)
XLA Ops:
  0.7 40.4 %shard_map.55 = f32[24,24,512]{2,1,0:T(8,128)S(1)} custom-call(f32[1]{0:T(128)} %bitcast.4.om_ref, f32[24,24,512]{2,1,0:T(8,128)} %f_hbm.1, f32[24,24,512]{2,1,0:T(8,128)} %u_hbm.1, f32[24,24]{1,0:T(8,128)} %kap_hbm.1, bf16[900,576]{1,0:T(8,128)(2,1)} %bitcast.5), custom_call_target="tpu_custom_call" | custom-call | tf_op jit(solution)/shard_map/pallas_call | solution.py:627
  41.0 1.0 %copy.7 = f32[24,24,512]{2,1,0:T(8,128)} copy(f32[24,24,512]{2,1,0:T(8,128)S(1)} %shard_map.55) | data formatting | bytes 2359296

commit v8 on v7

--- a/solution.py
+++ b/solution.py
@@ -495,21 +495,23 @@
     def towards(way):
         return jnp.where(way == 0, has_up, has_dn), jnp.where(way == 0, up_row, dn_row)
 
-    def late_next(t, ch, ahead):
-        for n, way in enumerate((1 - slow, slow)):
-            present, r_to = towards(way)
-
-            @pl.when(present)
-            def _():
-                z_copy(t, ch, 1 - way, r_to).wait_recv()
-                v_sc[ch, pl.ds(way * (band + sub), band), left:left + wide] = z_recv[1 - way, t, ch].astype(F32)
-
-            e_late[pl.ds(way * band, band), :, in_lanes(ch)] = update(ch, way * (ext - band), band).astype(BF16)
-            if n == 0 and ahead:
-                first = slow * (sub - band)
-                rows = pl.ds(pl.multiple_of(first * sub, 32), band * sub)
-                for side in range(2):
-                    acc[side, rows, in_lanes(ch)] = solve(in_lanes(ch), side, first, band, way).reshape(band * sub, LANES)
+    def late_part(t, ch, way):
+        present, r_to = towards(way)
+
+        @pl.when(present)
+        def _():
+            z_copy(t, ch, 1 - way, r_to).wait_recv()
+            v_sc[ch, pl.ds(way * (band + sub), band), left:left + wide] = z_recv[1 - way, t, ch].astype(F32)
+
+        e_late[pl.ds(way * band, band), :, in_lanes(ch)] = update(ch, way * (ext - band), band).astype(BF16)
+
+    def late_next(t, ch):
+        late_part(t, ch, 1 - slow)
+        first = slow * (sub - band)
+        rows = pl.ds(pl.multiple_of(first * sub, 32), band * sub)
+        for side in range(2):
+            acc[side, rows, in_lanes(ch)] = solve(in_lanes(ch), side, first, band, 1 - slow).reshape(band * sub, LANES)
+        late_part(t, ch, slow)
 
     def solve(lanes, side, first, count, only=None):
         n = count * sub
@@ -572,7 +574,7 @@
             far_wait()
             far_residual()
         for ch in range(chunks):
-            late_next(t, ch, True)
+            late_next(t, ch)
             solve_and_send(t + 1, ch, slow)
         interior()
         return carry
@@ -588,13 +590,17 @@
             device_id=(other, row), device_id_type=MESH)
 
     for ch in range(chunks):
-        late_next(SWEEPS - 2, ch, False)
+        late_part(SWEEPS - 2, ch, 1 - slow)
+    for side in range(2):
+        acc[side] = solve(slice(0, half), side, 0, sub, 1 - slow).reshape(sub * sub, half)
+    for ch in range(chunks):
+        late_part(SWEEPS - 2, ch, slow)
         for n in range(2):
             first, past = cuts[n], cuts[n + 1]
-            z = solve(in_lanes(ch), other, first, past - first).astype(BF16).astype(F32)
+            z = solve(in_lanes(ch), other, first, past - first, slow).astype(BF16).astype(F32)
             u_fin[ch, first:past] = u_sc[ch, first:past, other_cols] + omega * z
             out_pair(ch, n, mine).start()
-    z_own = solve(slice(0, half), col, 0, sub).astype(BF16).astype(F32)
+    z_own = solve(slice(0, half), col, 0, sub, slow).astype(BF16).astype(F32)
     for ch in range(chunks):
         out_ref[:, :, lanes_of(mine, ch)] = u_sc[ch, :, my_cols] + omega * z_own[:, :, in_lanes(ch)]
 

time: 42.2 us -> 42.2 us (level)
  no operation moved by 1% of the time
where the time goes in v8:
time: 42.2 us; the launch traced here: 42.1 us
  Pallas kernels  40.4 us (96%)
  local copies, waits for them, and re-layouts  1.02 us (2%)
  between operations  0.66 us (2%)
    pallas_call x1, Pallas kernels, device_fn(): pl.pallas_call(functools.partial(kernel, row_count, sub, halo, chunks), o...  40.4 us
    unnamed x1, local copies, waits for them, and re-layouts  1.02 us

profile of v8, /device:TPU:97, one launch (start us, length us, event | category | flops | bytes accessed | tf_op | source)
XLA Modules:
  0.0 42.1 jit_solution(642473766513932632)
XLA Ops:
  0.7 40.4 %shard_map.55 = f32[24,24,512]{2,1,0:T(8,128)S(1)} custom-call(f32[1]{0:T(128)} %bitcast.4.om_ref, f32[24,24,512]{2,1,0:T(8,128)} %f_hbm.1, f32[24,24,512]{2,1,0:T(8,128)} %u_hbm.1, f32[24,24]{1,0:T(8,128)} %kap_hbm.1, bf16[900,576]{1,0:T(8,128)(2,1)} %bitcast.5), custom_call_target="tpu_custom_call" | custom-call | tf_op jit(solution)/shard_map/pallas_call | solution.py:633
  41.0 1.0 %copy.7 = f32[24,24,512]{2,1,0:T(8,128)} copy(f32[24,24,512]{2,1,0:T(8,128)S(1)} %shard_map.55) | data formatting | bytes 2359296
